TPU v7x, 128 devices: a whole 4x4x4 slice. The times are simulated.
128 devices in a mesh: lat: 16 (over z, y_lo, core), lon: 8 (over y_hi, x).
Axes of the slice: x: 4, y: 4 (y_hi: 2, y_lo: 2; y = y_hi * 2 + y_lo), z: 4, core: 2. Of those that a mesh axis runs over, the one named last changes fastest.
Arguments:
- field: bfloat16 [256, 256, 256], P('lat', 'lon'), may hold values from -6 to 6
- weights: bfloat16 [16, 8, 3072, 3072], P('lat', 'lon'), may hold values from -0.09375 to 0.09375
- strip_ids: int32 [16, 8], P('lat'), may hold values from 0 to 63, as said below
- counts: int32 [16], P('lat'), may hold values from 2 to 8, as said below
Outputs:
- remapped: bfloat16 [131072, 256], P(('lat', 'lon'))
Inputs may be any that keep to these rules, and one draw needn't show every extreme that they name: `strip_ids`: row b holds consecutive global strip numbers, the last one repeated where the run meets the end of its window, all among the strips of source bands b - 2 to b + 2, band c holding strips 4 * c to 4 * c + 3. Band b uses the first counts[b] slots of its row.
All inputs are finite; a program needn't handle non-finite values.
Results may differ from a plain program's by a relative error of at most 0.0059.
Values may be sent and summed in bfloat16 or wider, within the bound.
No kernel may reach another device: no remote copies, remote signals or barrier semaphores. Data moves between devices by JAX's collectives and lax.ppermute only.
A program may use at most 64 MiB of HBM per device.

v0:
```python
import jax
import jax.numpy as jnp
from jax import lax
from jax.sharding import PartitionSpec as P

STRIP_ROWS = 4
SLOTS = 8
REACH = 2


def extended(cells, sides, width, closed):
    for axis, dim in sides:
        count = lax.axis_size(axis)
        ends = count if closed else count - 1
        head = lax.slice_in_dim(cells, 0, width, axis=dim)
        tail = lax.slice_in_dim(cells, cells.shape[dim] - width, cells.shape[dim], axis=dim)
        cells = jnp.concatenate(
            [
                lax.ppermute(tail, axis, [(i, (i + 1) % count) for i in range(ends)]),
                cells,
                lax.ppermute(head, axis, [((i + 1) % count, i) for i in range(ends)]),
            ],
            axis=dim,
        )
    return cells


def from_behind(block, axis, distance):
    devices = range(lax.axis_size(axis))
    route = [(i - distance, i) for i in devices if i - distance in devices]
    return lax.ppermute(block, axis, route)


def passed_along(block, axis, distance):
    devices = range(lax.axis_size(axis))
    route = [((i - distance) % len(devices), i) for i in devices]
    return lax.ppermute(block, axis, route)


def strip_stack(padded, strip_rows):
    values = padded.astype(jnp.float32)
    centre = padded[1:-1, 1:-1]
    eastward = ((values[1:-1, 2:] - values[1:-1, :-2]) * 0.5).astype(jnp.bfloat16)
    northward = ((values[2:, 1:-1] - values[:-2, 1:-1]) * 0.5).astype(jnp.bfloat16)
    row_count, lon_count, chan_count = centre.shape
    components = [
        component.reshape(row_count // strip_rows, strip_rows, lon_count, chan_count)
        for component in (centre, eastward, northward)
    ]
    stacked = jnp.stack(components, axis=1)
    return stacked.reshape(row_count // strip_rows, 3 * strip_rows * lon_count, chan_count)


def body(field, weights, strip_ids, counts):
    lon_padded = extended(field, (("lon", 1),), 1, True)
    both_padded = extended(lon_padded, (("lat", 0),), 1, False)
    band_index = lax.axis_index("lat")
    band_count = lax.axis_size("lat")
    upper_ghost = jnp.where(band_index == 0, lon_padded[:1], both_padded[:1])
    lower_ghost = jnp.where(band_index == band_count - 1, lon_padded[-1:], both_padded[-1:])
    padded = jnp.concatenate([upper_ghost, both_padded[1:-1], lower_ghost], axis=0)
    own_strips = strip_stack(padded, STRIP_ROWS)
    per_device = own_strips.shape[0]
    gathered = []
    for reach_step in range(-REACH, REACH + 1):
        if reach_step == 0:
            gathered.append(own_strips)
        else:
            remote_tile = from_behind(padded, "lat", -reach_step)
            gathered.append(strip_stack(remote_tile, STRIP_ROWS))
    neighbourhood = jnp.concatenate(gathered, axis=0)
    local_ids = strip_ids[0] - (band_index - REACH) * per_device
    live_slots = jnp.arange(SLOTS, dtype=jnp.int32) < counts[0]
    picked = jnp.take(neighbourhood, local_ids, axis=0)
    picked = jnp.where(live_slots[:, None, None], picked, jnp.zeros_like(picked))
    slot_width = picked.shape[1]
    chan_count = picked.shape[2]
    picked = picked.reshape(SLOTS * slot_width, chan_count)
    partial_sums = jnp.dot(weights[0, 0], picked, preferred_element_type=jnp.float32)
    sector_rows = partial_sums.shape[0] // 3
    from_west = passed_along(partial_sums[2 * sector_rows :].astype(jnp.bfloat16), "lon", 1).astype(
        jnp.float32
    )
    from_east = passed_along(partial_sums[:sector_rows].astype(jnp.bfloat16), "lon", -1).astype(
        jnp.float32
    )
    total = partial_sums[sector_rows : 2 * sector_rows] + from_west + from_east
    return total.astype(jnp.bfloat16)


def solution(mesh):
    placed = (P("lat", "lon", None), P("lat", "lon", None, None), P("lat", None), P("lat"))
    return jax.shard_map(
        body, mesh=mesh, in_specs=placed, out_specs=P(("lat", "lon"), None), check_vma=False
    )
```

profile of v0, /device:TPU:38, one launch (start us, length us, event | category | flops | bytes accessed | tf_op | source)
XLA Modules:
  0.0 86.4 jit_solution(2380271061009193182)
XLA Ops:
  0.0 0.9 %fusion.30 = (bf16[16,1,256]{2,1,0:T(2,128)(2,1)S(1)}, bf16[16,1,256]{2,1,0:T(2,128)(2,1)S(1)}) fusion(bf16[16,32,256]{2,1,0:T(8,128)(2,1)} %param.4), kind=kLoop, calls=%fused_computation.62 | loop fusion | bytes 32768 | tf_op jit(solution)/shard_map/slice | solution.py:16
  0.9 3.2 %collective-permute-start = (bf16[16,1,256]{2,1,0:T(2,128)(2,1)S(1)}, bf16[16,1,256]{2,1,0:T(2,128)(2,1)S(1)}, u32[]{:S(2)}, u32[]{:S(2)}) collective-permute-start(bf16[16,1,256]{2,1,0:T(2,128)(2,1)S(1)} %get-tuple-element.21), channel_id=1, source_target_pairs={{0,1},{1,2},{2,3},{3,4},{4,5},{5,6},{6,7},{7,0},{8,9},{9,10},{10,1... | collective-permute-start | bytes 24584 | tf_op jit(solution)/shard_map/ppermute | solution.py:19
  5.6 5.9 %collective-permute-done.1 = bf16[16,1,256]{2,1,0:T(2,128)(2,1)S(1)} collective-permute-done((bf16[16,1,256]{2,1,0:T(2,128)(2,1)S(1)}, bf16[16,1,256]{2,1,0:T(2,128)(2,1)S(1)}, u32[]{:S(2)}, u32[]{:S(2)}) %collective-permute-start.1) | collective-permute-done | bytes 8224 | tf_op jit(solution)/shard_map/ppermute | solution.py:21
  12.2 1.9 %collective-permute-start.2 = (bf16[1,34,256]{2,1,0:T(8,128)(2,1)S(1)}, bf16[1,34,256]{2,1,0:T(8,128)(2,1)S(1)}, u32[]{:S(2)}, u32[]{:S(2)}) collective-permute-start(bf16[1,34,256]{2,1,0:T(8,128)(2,1)S(1)} %pad_maximum_fusion.6), channel_id=1, source_target_pairs={{0,8},{8,16},{16,24},{24,32},{32,40},{40,48},{48,56},{56,64},{64,7... | collective-permute-start | bytes 52232 | tf_op jit(solution)/shard_map/ppermute | solution.py:19
  14.8 3.4 %collective-permute-done.2 = bf16[1,34,256]{2,1,0:T(8,128)(2,1)S(1)} collective-permute-done((bf16[1,34,256]{2,1,0:T(8,128)(2,1)S(1)}, bf16[1,34,256]{2,1,0:T(8,128)(2,1)S(1)}, u32[]{:S(2)}, u32[]{:S(2)}) %collective-permute-start.2) | collective-permute-done | bytes 17440 | tf_op jit(solution)/shard_map/ppermute | solution.py:19
  18.9 1.9 %collective-permute-start.3 = (bf16[1,34,256]{2,1,0:T(8,128)(2,1)S(1)}, bf16[1,34,256]{2,1,0:T(8,128)(2,1)S(1)}, u32[]{:S(2)}, u32[]{:S(2)}) collective-permute-start(bf16[1,34,256]{2,1,0:T(8,128)(2,1)S(1)} %get-tuple-element.6), channel_id=1, source_target_pairs={{8,0},{16,8},{24,16},{32,24},{40,32},{48,40},{56,48},{64,56},{72,6... | collective-permute-start | bytes 52232 | tf_op jit(solution)/shard_map/ppermute | solution.py:21
  20.9 1.4 %collective-permute-done.3 = bf16[1,34,256]{2,1,0:T(8,128)(2,1)S(1)} collective-permute-done((bf16[1,34,256]{2,1,0:T(8,128)(2,1)S(1)}, bf16[1,34,256]{2,1,0:T(8,128)(2,1)S(1)}, u32[]{:S(2)}, u32[]{:S(2)}) %collective-permute-start.3) | collective-permute-done | bytes 17440 | tf_op jit(solution)/shard_map/ppermute | solution.py:21
  22.3 1.1 %fusion.28 = (f32[18,34,256]{2,1,0:T(8,128)S(1)}, bf16[18,34,256]{2,1,0:T(8,128)(2,1)S(1)}) fusion(bf16[1,34,256]{2,1,0:T(8,128)(2,1)S(1)} %broadcast_select_fusion, bf16[16,1,256]{2,1,0:T(2,128)(2,1)S(1)} %collective-permute-done.1, bf16[16,32,256]{2,1,0:T(8,128)(2,1)} %param.4, bf16[16,1,256]{2,1,0:T(2,128)(2,1)S(1)} %collective-permute-done, ...), kind=kLoop, calls=%fused_computation.60 | loop fusion | flops 1723392 | bytes 1253376 | tf_op jit(solution)/shard_map/convert_element_type | solution.py:41
  23.4 1.9 %collective-permute-start.5 = (bf16[18,34,256]{2,1,0:T(8,128)(2,1)S(1)}, bf16[18,34,256]{2,1,0:T(8,128)(2,1)S(1)}, u32[]{:S(2)}, u32[]{:S(2)}) collective-permute-start(bf16[18,34,256]{2,1,0:T(8,128)(2,1)S(1)} %get-tuple-element.20), channel_id=1, source_target_pairs={{0,8},{8,16},{16,24},{24,32},{32,40},{40,48},{48,56},{56,64},{64,7... | collective-permute-start | bytes 940040 | tf_op jit(solution)/shard_map/ppermute | solution.py:31
  25.4 5.4 %collective-permute-start.4 = (bf16[18,34,256]{2,1,0:T(8,128)(2,1)S(1)}, bf16[18,34,256]{2,1,0:T(8,128)(2,1)S(1)}, u32[]{:S(2)}, u32[]{:S(2)}) collective-permute-start(bf16[18,34,256]{2,1,0:T(8,128)(2,1)S(1)} %get-tuple-element.20), channel_id=1, source_target_pairs={{0,16},{8,24},{16,32},{24,40},{32,48},{40,56},{48,64},{56,72},{64,... | collective-permute-start | bytes 940040 | tf_op jit(solution)/shard_map/ppermute | solution.py:31
  30.7 1.9 %collective-permute-start.6 = (bf16[18,34,256]{2,1,0:T(8,128)(2,1)S(1)}, bf16[18,34,256]{2,1,0:T(8,128)(2,1)S(1)}, u32[]{:S(2)}, u32[]{:S(2)}) collective-permute-start(bf16[18,34,256]{2,1,0:T(8,128)(2,1)S(1)} %get-tuple-element.20), channel_id=1, source_target_pairs={{8,0},{16,8},{24,16},{32,24},{40,32},{48,40},{56,48},{64,56},{72,6... | collective-permute-start | bytes 940040 | tf_op jit(solution)/shard_map/ppermute | solution.py:31
  32.7 2.8 %collective-permute-start.7 = (bf16[18,34,256]{2,1,0:T(8,128)(2,1)S(1)}, bf16[18,34,256]{2,1,0:T(8,128)(2,1)S(1)}, u32[]{:S(2)}, u32[]{:S(2)}) collective-permute-start(bf16[18,34,256]{2,1,0:T(8,128)(2,1)S(1)} %get-tuple-element.20), channel_id=1, source_target_pairs={{16,0},{24,8},{32,16},{40,24},{48,32},{56,40},{64,48},{72,56},{80,... | collective-permute-start | bytes 940040 | tf_op jit(solution)/shard_map/ppermute | solution.py:31
  36.0 3.7 %collective-permute-done.4 = bf16[18,34,256]{2,1,0:T(8,128)(2,1)S(1)} collective-permute-done((bf16[18,34,256]{2,1,0:T(8,128)(2,1)S(1)}, bf16[18,34,256]{2,1,0:T(8,128)(2,1)S(1)}, u32[]{:S(2)}, u32[]{:S(2)}) %collective-permute-start.4) | collective-permute-done | bytes 313376 | tf_op jit(solution)/shard_map/ppermute | solution.py:31
  41.0 5.6 %collective-permute-done.6 = bf16[18,34,256]{2,1,0:T(8,128)(2,1)S(1)} collective-permute-done((bf16[18,34,256]{2,1,0:T(8,128)(2,1)S(1)}, bf16[18,34,256]{2,1,0:T(8,128)(2,1)S(1)}, u32[]{:S(2)}, u32[]{:S(2)}) %collective-permute-start.6) | collective-permute-done | bytes 313376 | tf_op jit(solution)/shard_map/ppermute | solution.py:31
  46.9 6.5 %collective-permute-done.7 = bf16[18,34,256]{2,1,0:T(8,128)(2,1)S(1)} collective-permute-done((bf16[18,34,256]{2,1,0:T(8,128)(2,1)S(1)}, bf16[18,34,256]{2,1,0:T(8,128)(2,1)S(1)}, u32[]{:S(2)}, u32[]{:S(2)}) %collective-permute-start.7) | collective-permute-done | bytes 313376 | tf_op jit(solution)/shard_map/ppermute | solution.py:31
  53.8 1.0 %constant_dynamic-update-slice_fusion.3 = bf16[20,384,256]{2,1,0:T(8,128)(2,1)} fusion(bf16[20,384,256]{2,1,0:T(8,128)(2,1)} %constant_dynamic-update-slice_fusion.4, bf16[4,384,256]{2,1,0:T(8,128)(2,1)S(1)} %bitcast.41), kind=kLoop, calls=%fused_computation.52 | loop fusion | bytes 1572864
  55.8 0.9 %constant_dynamic-update-slice_fusion.1 = bf16[20,384,256]{2,1,0:T(8,128)(2,1)} fusion(bf16[20,384,256]{2,1,0:T(8,128)(2,1)} %constant_dynamic-update-slice_fusion.2, bf16[4,384,256]{2,1,0:T(8,128)(2,1)S(1)} %bitcast.42), kind=kLoop, calls=%fused_computation.50 | loop fusion | bytes 1572864
  57.0 0.9 %constant_dynamic-update-slice_fusion = bf16[20,384,256]{2,1,0:T(8,128)(2,1)} fusion(bf16[20,384,256]{2,1,0:T(8,128)(2,1)} %constant_dynamic-update-slice_fusion.1, bf16[4,384,256]{2,1,0:T(8,128)(2,1)S(1)} %bitcast.43), kind=kLoop, calls=%fused_computation.49 | loop fusion | bytes 1572864 | tf_op jit(solution)/shard_map/concatenate | solution.py:71
  57.9 2.8 %gather_fusion = bf16[8,384,256]{2,1,0:T(8,128)(2,1)S(1)} fusion(bf16[20,384,256]{2,1,0:T(8,128)(2,1)} %constant_dynamic-update-slice_fusion, s32[1024]{0:T(1024)S(1)} %pad_clamp_fusion), kind=kCustom, calls=%fused_computation | custom fusion | bytes 3145760 | tf_op jit(solution)/shard_map/jit(_take)/gather | solution.py:74
  60.9 9.1 %fusion.31 = (bf16[3072,256]{0,1:T(8,128)(2,1)S(1)}, f32[3072,256]{0,1:T(8,128)S(1)}) fusion(bf16[3072,256]{1,0:T(8,128)(2,1)S(1)} %bitcast.45, bf16[1,1,3072,3072]{3,2,1,0:T(8,128)(2,1)} %param.5), kind=kOutput, calls=%fused_computation.63 | convolution fusion | flops 4832624640 | bytes 25165824 | tf_op jit(solution)/shard_map/dot_general | solution.py:79
  70.1 2.0 %collective-permute-start.9 = (bf16[1024,256]{0,1:T(8,128)(2,1)S(1)}, bf16[1024,256]{0,1:T(8,128)(2,1)S(1)}, u32[]{:S(2)}, u32[]{:S(2)}) collective-permute-start(bf16[1024,256]{0,1:T(8,128)(2,1)S(1)} %get-tuple-element.8), channel_id=1, source_target_pairs={{1,0},{2,1},{3,2},{4,3},{5,4},{6,5},{7,6},{0,7},{9,8},{10,9},{11,1... | collective-permute-start | bytes 1572872 | tf_op jit(solution)/shard_map/ppermute | solution.py:37
  72.1 9.3 %collective-permute-done.8 = bf16[1024,256]{0,1:T(8,128)(2,1)S(1)} collective-permute-done((bf16[1024,256]{0,1:T(8,128)(2,1)S(1)}, bf16[1024,256]{0,1:T(8,128)(2,1)S(1)}, u32[]{:S(2)}, u32[]{:S(2)}) %collective-permute-start.8) | collective-permute-done | bytes 524320 | tf_op jit(solution)/shard_map/ppermute | solution.py:37
  81.5 3.7 %collective-permute-done.9 = bf16[1024,256]{0,1:T(8,128)(2,1)S(1)} collective-permute-done((bf16[1024,256]{0,1:T(8,128)(2,1)S(1)}, bf16[1024,256]{0,1:T(8,128)(2,1)S(1)}, u32[]{:S(2)}, u32[]{:S(2)}) %collective-permute-start.9) | collective-permute-done | bytes 524320 | tf_op jit(solution)/shard_map/ppermute | solution.py:37
  85.4 1.0 %copy.6 = bf16[1024,256]{1,0:T(8,128)(2,1)} copy(bf16[1024,256]{0,1:T(8,128)(2,1)S(1)} %fusion.6) | data formatting | bytes 1048576 | tf_op jit(solution)/shard_map/convert_element_type | solution.py:88
  (35 shorter events, 7.2 us)
Async XLA Ops:
  0.0 35.7 %copy-start = (bf16[16,32,256]{2,1,0:T(8,128)(2,1)S(1)}, bf16[16,32,256]{2,1,0:T(8,128)(2,1)}, u32[]{:S(2)}) copy-start(bf16[16,32,256]{2,1,0:T(8,128)(2,1)} %param.4) | copy-start | bytes 786436
  0.9 4.6 %collective-permute-start = (bf16[16,1,256]{2,1,0:T(2,128)(2,1)S(1)}, bf16[16,1,256]{2,1,0:T(2,128)(2,1)S(1)}, u32[]{:S(2)}, u32[]{:S(2)}) collective-permute-start(bf16[16,1,256]{2,1,0:T(2,128)(2,1)S(1)} %get-tuple-element.21), channel_id=1, source_target_pairs={{0,1},{1,2},{2,3},{3,4},{4,5},{5,6},{6,7},{7,0},{8,9},{9,10},{10,1... | collective-permute-start | bytes 24584 | tf_op jit(solution)/shard_map/ppermute | solution.py:19
  4.1 7.4 %collective-permute-start.1 = (bf16[16,1,256]{2,1,0:T(2,128)(2,1)S(1)}, bf16[16,1,256]{2,1,0:T(2,128)(2,1)S(1)}, u32[]{:S(2)}, u32[]{:S(2)}) collective-permute-start(bf16[16,1,256]{2,1,0:T(2,128)(2,1)S(1)} %get-tuple-element.22), channel_id=1, source_target_pairs={{1,0},{2,1},{3,2},{4,3},{5,4},{6,5},{7,6},{0,7},{9,8},{10,9},{11,1... | collective-permute-start | bytes 24584 | tf_op jit(solution)/shard_map/ppermute | solution.py:21
  12.2 6.0 %collective-permute-start.2 = (bf16[1,34,256]{2,1,0:T(8,128)(2,1)S(1)}, bf16[1,34,256]{2,1,0:T(8,128)(2,1)S(1)}, u32[]{:S(2)}, u32[]{:S(2)}) collective-permute-start(bf16[1,34,256]{2,1,0:T(8,128)(2,1)S(1)} %pad_maximum_fusion.6), channel_id=1, source_target_pairs={{0,8},{8,16},{16,24},{24,32},{32,40},{40,48},{48,56},{56,64},{64,7... | collective-permute-start | bytes 52232 | tf_op jit(solution)/shard_map/ppermute | solution.py:19
  18.9 3.4 %collective-permute-start.3 = (bf16[1,34,256]{2,1,0:T(8,128)(2,1)S(1)}, bf16[1,34,256]{2,1,0:T(8,128)(2,1)S(1)}, u32[]{:S(2)}, u32[]{:S(2)}) collective-permute-start(bf16[1,34,256]{2,1,0:T(8,128)(2,1)S(1)} %get-tuple-element.6), channel_id=1, source_target_pairs={{8,0},{16,8},{24,16},{32,24},{40,32},{48,40},{56,48},{64,56},{72,6... | collective-permute-start | bytes 52232 | tf_op jit(solution)/shard_map/ppermute | solution.py:21
  23.4 12.4 %collective-permute-start.5 = (bf16[18,34,256]{2,1,0:T(8,128)(2,1)S(1)}, bf16[18,34,256]{2,1,0:T(8,128)(2,1)S(1)}, u32[]{:S(2)}, u32[]{:S(2)}) collective-permute-start(bf16[18,34,256]{2,1,0:T(8,128)(2,1)S(1)} %get-tuple-element.20), channel_id=1, source_target_pairs={{0,8},{8,16},{16,24},{24,32},{32,40},{40,48},{48,56},{56,64},{64,7... | collective-permute-start | bytes 940040 | tf_op jit(solution)/shard_map/ppermute | solution.py:31
  25.4 14.3 %collective-permute-start.4 = (bf16[18,34,256]{2,1,0:T(8,128)(2,1)S(1)}, bf16[18,34,256]{2,1,0:T(8,128)(2,1)S(1)}, u32[]{:S(2)}, u32[]{:S(2)}) collective-permute-start(bf16[18,34,256]{2,1,0:T(8,128)(2,1)S(1)} %get-tuple-element.20), channel_id=1, source_target_pairs={{0,16},{8,24},{16,32},{24,40},{32,48},{40,56},{48,64},{56,72},{64,... | collective-permute-start | bytes 940040 | tf_op jit(solution)/shard_map/ppermute | solution.py:31
  30.7 15.9 %collective-permute-start.6 = (bf16[18,34,256]{2,1,0:T(8,128)(2,1)S(1)}, bf16[18,34,256]{2,1,0:T(8,128)(2,1)S(1)}, u32[]{:S(2)}, u32[]{:S(2)}) collective-permute-start(bf16[18,34,256]{2,1,0:T(8,128)(2,1)S(1)} %get-tuple-element.20), channel_id=1, source_target_pairs={{8,0},{16,8},{24,16},{32,24},{40,32},{48,40},{56,48},{64,56},{72,6... | collective-permute-start | bytes 940040 | tf_op jit(solution)/shard_map/ppermute | solution.py:31
  32.7 20.7 %collective-permute-start.7 = (bf16[18,34,256]{2,1,0:T(8,128)(2,1)S(1)}, bf16[18,34,256]{2,1,0:T(8,128)(2,1)S(1)}, u32[]{:S(2)}, u32[]{:S(2)}) collective-permute-start(bf16[18,34,256]{2,1,0:T(8,128)(2,1)S(1)} %get-tuple-element.20), channel_id=1, source_target_pairs={{16,0},{24,8},{32,16},{40,24},{48,32},{56,40},{64,48},{72,56},{80,... | collective-permute-start | bytes 940040 | tf_op jit(solution)/shard_map/ppermute | solution.py:31
  70.1 11.4 %collective-permute-start.8 = (bf16[1024,256]{0,1:T(8,128)(2,1)S(1)}, bf16[1024,256]{0,1:T(8,128)(2,1)S(1)}, u32[]{:S(2)}, u32[]{:S(2)}) collective-permute-start(bf16[1024,256]{0,1:T(8,128)(2,1)S(1)} %get-tuple-element.7), channel_id=1, source_target_pairs={{7,0},{0,1},{1,2},{2,3},{3,4},{4,5},{5,6},{6,7},{15,8},{8,9},{9,10... | collective-permute-start | bytes 1572872 | tf_op jit(solution)/shard_map/ppermute | solution.py:37
  70.1 15.0 %collective-permute-start.9 = (bf16[1024,256]{0,1:T(8,128)(2,1)S(1)}, bf16[1024,256]{0,1:T(8,128)(2,1)S(1)}, u32[]{:S(2)}, u32[]{:S(2)}) collective-permute-start(bf16[1024,256]{0,1:T(8,128)(2,1)S(1)} %get-tuple-element.8), channel_id=1, source_target_pairs={{1,0},{2,1},{3,2},{4,3},{5,4},{6,5},{7,6},{0,7},{9,8},{10,9},{11,1... | collective-permute-start | bytes 1572872 | tf_op jit(solution)/shard_map/ppermute | solution.py:37
where the time goes:
time: 86.9 us; the launch traced here: 86.4 us
  waiting for transfers between devices  39.7 us (46%)
  starting transfers between devices  21.2 us (24%)
  local copies, waits for them, and re-layouts  9.8 us (11%)
  matrix products  9.06 us (10%)
  other arithmetic  5.81 us (7%)
  between operations  0.9 us (1%)
    ppermute x4, waiting for transfers between devices, from_behind(): return lax.ppermute(block, axis, route)  15.8 us
    ppermute x2, waiting for transfers between devices, passed_along(): return lax.ppermute(block, axis, route)  13 us
    ppermute x4, starting transfers between devices, from_behind(): return lax.ppermute(block, axis, route)  12 us
    dot_general x1, matrix products, body(): jnp.dot(weights[0, 0], picked, preferred_element_type=jnp.float32)  9.06 us
    ppermute x2, waiting for transfers between devices, extended(): lax.ppermute(head, axis, [((i + 1) % count, i) for i in range(ends)])  7.35 us
    ppermute x2, starting transfers between devices, extended(): lax.ppermute(tail, axis, [(i, (i + 1) % count) for i in range(ends)])  5.1 us
    unnamed x6, local copies, waits for them, and re-layouts  3.76 us
    ppermute x2, waiting for transfers between devices, extended(): lax.ppermute(tail, axis, [(i, (i + 1) % count) for i in range(ends)])  3.53 us
  transfers between devices with their start and end apart: 10, of which 9 were waited for; matrix products, arithmetic and copies ran while one was open for 4% of the time, Pallas kernels for 0%

commit v1 on v0

v1 whole, which is shorter than its diff:
```python
import jax
import jax.numpy as jnp
from jax import lax
from jax.experimental import pallas as pl
from jax.experimental.pallas import tpu as pltpu
from jax.sharding import PartitionSpec as P

STRIP_ROWS = 4
SLOTS = 8
REACH = 2
BF16 = jnp.bfloat16
F32 = jnp.float32


def swap(block, axis, partner):
    return lax.ppermute(block, axis, [(i, partner(i)) for i in range(lax.axis_size(axis))])


def near_chip(i):
    return i ^ 2


def far_chip(i, count=16):
    return (i + 2) % count if (i // 2) % 2 else (i - 2) % count


def load_body(meta, w, out, sem, *, which):
    size = out.shape[0]
    start = (jnp.where(meta[1] == 0, 0, 2 * size), jnp.where(meta[1] == 0, 2 * size, 0), size)[which]
    copy = pltpu.make_async_copy(w.at[pl.ds(start, size)], out, sem)
    copy.start()
    copy.wait()


def prep_body(meta, own, near, far, mate, beyond, own_cols, near_cols, far_cols, w, picked, out, rows, west, east):
    rows_per = own.shape[0]
    band = meta[0]
    core, odd = band % 2, (band // 2) % 2
    slot_of_near = jnp.where(odd == 1, 0, 2 * REACH)
    slot_of_far = 2 * REACH - slot_of_near
    slot_of_hop = jnp.where(core == 0, REACH - 1, REACH + 1)
    slot_of_mate = 2 * REACH - slot_of_hop

    def place(slot, tile, cols):
        rows[pl.ds(1 + slot * rows_per, rows_per)] = tile
        for i in range(rows_per):
            west[slot * rows_per + i] = cols[i : i + 1]
            east[slot * rows_per + i] = cols[rows_per + i : rows_per + i + 1]

    place(REACH, own[...], own_cols[...].astype(F32))
    place(slot_of_near, near[...], near_cols[...].astype(F32))
    place(slot_of_far, far[...], far_cols[...].astype(F32))
    place(slot_of_hop, mate[:rows_per], mate[2 * rows_per + 1].astype(F32))
    place(slot_of_mate, mate[rows_per : 2 * rows_per], mate[2 * rows_per + 2].astype(F32))
    last = (2 * REACH + 1) * rows_per + 1
    rows[jnp.where(core == 0, 0, last)] = beyond[0]
    rows[jnp.where(core == 0, last, 0)] = mate[2 * rows_per]

    @pl.when(band <= REACH)
    def _():
        edge = rows_per * (REACH - band)
        rows[edge] = rows[edge + 1]

    @pl.when(band >= meta[2] - 1 - REACH)
    def _():
        edge = rows_per * (meta[2] + REACH - band)
        rows[edge + 1] = rows[edge]

    lon, chan = own.shape[1], own.shape[2]
    cells = STRIP_ROWS * lon
    first_strip = (band - REACH) * (rows_per // STRIP_ROWS)
    place_in_row = lax.broadcasted_iota(jnp.int32, (STRIP_ROWS, lon, chan), 1)
    for k in range(SLOTS):
        base = STRIP_ROWS * (meta[4 + k] - first_strip)
        block = rows[pl.ds(base, STRIP_ROWS + 2)].astype(F32)
        centre = block[1:-1]
        north = (block[2:] - block[:-2]) * 0.5
        flat = centre.reshape(cells, chan)
        before = pltpu.roll(flat, 1, axis=0).reshape(centre.shape)
        after = pltpu.roll(flat, cells - 1, axis=0).reshape(centre.shape)
        before = jnp.where(place_in_row == 0, west[pl.ds(base, STRIP_ROWS)], before)
        after = jnp.where(place_in_row == lon - 1, east[pl.ds(base, STRIP_ROWS)], after)
        eastward = (after - before) * 0.5
        live = k < meta[3]
        for c, part in enumerate((centre, eastward, north)):
            start = (3 * k + c) * cells
            part = jnp.where(live, part.reshape(cells, chan), 0.0)
            picked[start : start + cells] = part.astype(BF16)
    out[...] = jnp.dot(w[...], picked[...], preferred_element_type=F32).astype(BF16)


def block_body(w, picked, out):
    out[...] = jnp.dot(w[...], picked[...], preferred_element_type=F32).astype(out.dtype)


def body(field, weights, strip_ids, counts):
    band, sector = lax.axis_index("lat"), lax.axis_index("lon")
    bands = lax.axis_size("lat")
    core, odd, parity = band % 2, (band // 2) % 2, sector % 2
    rows_per, lon, chan = field.shape
    near_lon = lambda i: i ^ 1
    far_lon = lambda i: (i + 1) % 8 if i % 2 else (i - 1) % 8

    far = swap(field, "lat", far_chip)
    near = swap(field, "lat", near_chip)
    edge_row = jnp.where(core == 1, field[-1:], field[:1])
    beyond = swap(edge_row, "lat", lambda i: (i + 3) % 16 if i % 2 else (i - 3) % 16)
    west_edge, east_edge = field[:, 0], field[:, -1]
    from_far = swap(jnp.where(parity == 0, west_edge, east_edge), "lon", far_lon)
    from_near = swap(jnp.where(parity == 0, east_edge, west_edge), "lon", near_lon)
    cols = jnp.where(
        parity == 0, jnp.concatenate([from_far, from_near]), jnp.concatenate([from_near, from_far])
    )
    far_cols = swap(cols, "lat", far_chip)
    near_cols = swap(cols, "lat", near_chip)
    pick_near = core == odd
    other_rows = jnp.where(
        core == 0,
        jnp.where(pick_near, far[-1:], near[-1:]),
        jnp.where(pick_near, far[:1], near[:1]),
    )
    message = jnp.concatenate(
        [
            jnp.where(pick_near, near, far),
            field,
            other_rows,
            jnp.where(pick_near, near_cols, far_cols)[None],
            cols[None],
        ]
    )
    mate = swap(message, "lat", lambda i: i ^ 1)

    meta = jnp.concatenate(
        [
            jnp.stack([band, parity, bands]).astype(jnp.int32),
            counts.astype(jnp.int32),
            strip_ids[0].astype(jnp.int32),
        ]
    )
    w = pltpu.with_memory_space_constraint(weights[0, 0], pltpu.HBM)
    size = w.shape[0] // 3
    width = w.shape[1]
    vmem = pl.BlockSpec(memory_space=pltpu.VMEM)
    smem = pl.BlockSpec(memory_space=pltpu.SMEM)
    held = lambda x: pltpu.with_memory_space_constraint(x, pltpu.VMEM)

    def load(which):
        return pl.pallas_call(
            lambda *refs: load_body(*refs, which=which),
            in_specs=[smem, pl.BlockSpec(memory_space=pltpu.HBM)],
            out_specs=vmem,
            out_shape=pltpu.VMEM((size, width), BF16),
            scratch_shapes=[pltpu.SemaphoreType.DMA],
            compiler_params=pltpu.CompilerParams(vmem_limit_bytes=1 << 20),
            cost_estimate=pl.CostEstimate(flops=1 << 32, transcendentals=0, bytes_accessed=2 * size * width),
            name="load",
        )(meta, w)

    w_far, w_near, w_own = held(load(0)), held(load(1)), held(load(2))
    halo = (2 * REACH + 1) * rows_per
    picked, to_far = pl.pallas_call(
        prep_body,
        in_specs=[smem] + [vmem] * 9,
        out_specs=[vmem, vmem],
        out_shape=[pltpu.VMEM((width, chan), BF16), pltpu.VMEM((size, chan), BF16)],
        scratch_shapes=[
            pltpu.VMEM((halo + 2, lon, chan), BF16),
            pltpu.VMEM((halo, 1, chan), F32),
            pltpu.VMEM((halo, 1, chan), F32),
        ],
        compiler_params=pltpu.CompilerParams(vmem_limit_bytes=16 << 20),
        name="prep",
    )(meta, field, near, far, mate, beyond, cols, near_cols, far_cols, w_far)
    picked = held(picked)

    def block(w_block, dtype, name):
        return pl.pallas_call(
            block_body,
            in_specs=[vmem, vmem],
            out_specs=vmem,
            out_shape=pltpu.VMEM((size, chan), dtype),
            compiler_params=pltpu.CompilerParams(vmem_limit_bytes=16 << 20),
            name=name,
        )(w_block, picked)

    got_far = swap(to_far, "lon", far_lon)
    got_near = swap(block(w_near, BF16, "side"), "lon", near_lon)
    own = block(w_own, F32, "own")
    return (own + got_far.astype(F32) + got_near.astype(F32)).astype(BF16)


def solution(mesh):
    placed = (P("lat", "lon", None), P("lat", "lon", None, None), P("lat", None), P("lat"))
    return jax.shard_map(
        body, mesh=mesh, in_specs=placed, out_specs=P(("lat", "lon"), None), check_vma=False
    )
```

time: 86.9 us -> 52.8 us (0.61)
  the two profiles are of different devices: /device:TPU:38 before, /device:TPU:1 now
where the time goes in v1:
time: 52.8 us; the launch traced here: 52.4 us
  starting transfers between devices  21.7 us (41%)
  Pallas kernels  16.2 us (31%)
  waiting for transfers between devices  9.23 us (17%)
  local copies, waits for them, and re-layouts  2.61 us (5%)
  other arithmetic  1.85 us (4%)
  between operations  0.82 us (2%)
    ppermute x10, starting transfers between devices, swap(): lax.ppermute(block, axis, [(i, partner(i)) for i in range(lax.axis_size(a...  21.7 us
    pallas_call x3, Pallas kernels, load(): pl.pallas_call(lambda *refs: load_body(*refs, which=which), in_specs=[sme...  10 us
    ppermute x10, waiting for transfers between devices, swap(): lax.ppermute(block, axis, [(i, partner(i)) for i in range(lax.axis_size(a...  9.23 us
    pallas_call x2, Pallas kernels, block(): pl.pallas_call(block_body, in_specs=[vmem, vmem], out_specs=vmem, out_sha...  3.58 us
    pallas_call x1, Pallas kernels, body(): pl.pallas_call(prep_body, in_specs=[smem] + [vmem] * 9, out_specs=[vmem,...  2.6 us
  transfers between devices with their start and end apart: 10, of which 4 were waited for; matrix products, arithmetic and copies ran while one was open for 7% of the time, Pallas kernels for 23%

profile of v1, /device:TPU:1, one launch (start us, length us, event | category | flops | bytes accessed | tf_op | source)
XLA Modules:
  0.0 52.4 jit_solution(7756382981332710867)
XLA Ops:
  0.0 2.1 %collective-permute-start = (bf16[16,32,256]{2,1,0:T(8,128)(2,1)}, bf16[16,32,256]{2,1,0:T(8,128)(2,1)S(1)}, u32[]{:S(2)}, u32[]{:S(2)}) collective-permute-start(bf16[16,32,256]{2,1,0:T(8,128)(2,1)} %own.2), channel_id=1, source_target_pairs={{0,16},{8,24},{16,0},{24,8},{32,48},{40,56},{48,32},{56,40},{64,80... | collective-permute-start | bytes 786440 | tf_op jit(solution)/shard_map/ppermute | solution.py:16
  2.1 3.6 %collective-permute-start.1 = (bf16[16,32,256]{2,1,0:T(8,128)(2,1)}, bf16[16,32,256]{2,1,0:T(8,128)(2,1)S(1)}, u32[]{:S(2)}, u32[]{:S(2)}) collective-permute-start(bf16[16,32,256]{2,1,0:T(8,128)(2,1)} %own.2), channel_id=1, source_target_pairs={{0,112},{8,120},{16,32},{24,40},{32,16},{40,24},{48,64},{56,72},{6... | collective-permute-start | bytes 786440 | tf_op jit(solution)/shard_map/ppermute | solution.py:16
  5.8 0.9 %fusion.3 = (bf16[16,1,256]{2,1,0:T(2,128)(2,1)S(1)}, bf16[16,1,256]{2,1,0:T(2,128)(2,1)S(1)}) fusion(bf16[16,32,256]{2,1,0:T(8,128)(2,1)} %own.2), kind=kLoop, calls=%fused_computation.14 | loop fusion | bytes 32768 | tf_op jit(solution)/shard_map/slice | solution.py:108
  6.7 5.2 %collective-permute-start.2 = (bf16[16,256]{1,0:T(8,128)(2,1)S(1)}, bf16[16,256]{1,0:T(8,128)(2,1)S(1)}, u32[]{:S(2)}, u32[]{:S(2)}) collective-permute-start(bf16[16,256]{1,0:T(8,128)(2,1)S(1)} %get-tuple-element.11), channel_id=1, source_target_pairs={{0,7},{1,2},{2,1},{3,4},{4,3},{5,6},{6,5},{7,0},{8,15},{9,10},{10,... | collective-permute-start | bytes 24584 | tf_op jit(solution)/shard_map/ppermute | solution.py:16
  11.9 0.7 %slice_select_fusion.2 = bf16[1,32,256]{2,1,0:T(8,128)(2,1)S(1)} fusion(bf16[16,32,256]{2,1,0:T(8,128)(2,1)} %own.2, pred[]{:T(512)S(6)} %eq.21), kind=kLoop, calls=%fused_computation.10 | loop fusion | flops 8192 | bytes 49153 | tf_op jit(solution)/shard_map/jit(_where)/select_n | solution.py:106
  13.3 0.7 %concatenate.34.refs_0_.meta = s32[12]{0:T(128)S(1)} concatenate(s32[1]{0:T(128)} %bitcast, s32[1]{0:T(128)} %bitcast.1, s32[1]{0:T(128)} %constant.43.clone.1, s32[1]{0:T(128)S(6)} %copy.17, s32[8]{0:T(128)} %bitcast.17), dimensions={0} | concatenate | bytes 96 | tf_op jit(solution)/shard_map/concatenate | solution.py:133
  14.0 0.6 %collective-permute-done.3 = bf16[16,256]{1,0:T(8,128)(2,1)S(1)} collective-permute-done((bf16[16,256]{1,0:T(8,128)(2,1)S(1)}, bf16[16,256]{1,0:T(8,128)(2,1)S(1)}, u32[]{:S(2)}, u32[]{:S(2)}) %collective-permute-start.3) | collective-permute-done | bytes 8224 | tf_op jit(solution)/shard_map/ppermute | solution.py:16
  14.7 0.7 %collective-permute-start.4 = (bf16[32,256]{1,0:T(8,128)(2,1)S(1)}, bf16[32,256]{1,0:T(8,128)(2,1)S(1)}, u32[]{:S(2)}, u32[]{:S(2)}) collective-permute-start(bf16[32,256]{1,0:T(8,128)(2,1)S(1)} %maximum_select_fusion.own_cols), channel_id=1, source_target_pairs={{0,16},{8,24},{16,0},{24,8},{32,48},{40,56},{48,32},{56,40},{64,80... | collective-permute-start | bytes 49160 | tf_op jit(solution)/shard_map/ppermute | solution.py:16
  15.4 3.9 %collective-permute-start.5 = (bf16[32,256]{1,0:T(8,128)(2,1)S(1)}, bf16[32,256]{1,0:T(8,128)(2,1)S(1)}, u32[]{:S(2)}, u32[]{:S(2)}) collective-permute-start(bf16[32,256]{1,0:T(8,128)(2,1)S(1)} %maximum_select_fusion.own_cols), channel_id=1, source_target_pairs={{0,112},{8,120},{16,32},{24,40},{32,16},{40,24},{48,64},{56,72},{6... | collective-permute-start | bytes 49160 | tf_op jit(solution)/shard_map/ppermute | solution.py:16
  19.4 0.1 select_dynamic-update-slice_fusion
  19.5 1.0 %constant_dynamic-update-slice_fusion = bf16[35,32,256]{2,1,0:T(8,128)(2,1)S(1)} fusion(bf16[35,32,256]{2,1,0:T(8,128)(2,1)S(1)} %select_dynamic-update-slice_fusion, bf16[16,32,256]{2,1,0:T(8,128)(2,1)} %own.2), kind=kLoop, calls=%fused_computation.11 | loop fusion | bytes 524288
  20.5 0.2 collective-permute-done.5.far_cols
  20.7 2.4 %collective-permute-start.6 = (bf16[35,32,256]{2,1,0:T(8,128)(2,1)S(1)}, bf16[35,32,256]{2,1,0:T(8,128)(2,1)S(1)}, u32[]{:S(2)}, u32[]{:S(2)}) collective-permute-start(bf16[35,32,256]{2,1,0:T(8,128)(2,1)S(1)} %fusion.2), channel_id=1, source_target_pairs={{0,8},{8,0},{16,24},{24,16},{32,40},{40,32},{48,56},{56,48},{64,72... | collective-permute-start | bytes 1720328 | tf_op jit(solution)/shard_map/ppermute | solution.py:16
  23.1 3.3 %load.4.w = bf16[1024,3072]{1,0:T(8,128)(2,1)S(1)} custom-call(s32[12]{0:T(128)S(1)} %concatenate.34.refs_0_.meta, bf16[3072,3072]{1,0:T(8,128)(2,1)} %bitcast.12), custom_call_target="tpu_custom_call" | custom-call | flops 4294967296 | bytes 6291456 | tf_op jit(solution)/shard_map/load/pallas_call | solution.py:148
  26.5 3.3 %load.5.w = bf16[1024,3072]{1,0:T(8,128)(2,1)S(1)} custom-call(s32[12]{0:T(128)S(1)} %concatenate.34.refs_0_.meta, bf16[3072,3072]{1,0:T(8,128)(2,1)} %bitcast.13), custom_call_target="tpu_custom_call" | custom-call | flops 4294967296 | bytes 6291456 | tf_op jit(solution)/shard_map/load/pallas_call | solution.py:148
  29.8 2.6 %prep.1 = (bf16[3072,256]{1,0:T(8,128)(2,1)S(1)}, bf16[1024,256]{1,0:T(8,128)(2,1)S(1)}) custom-call(s32[12]{0:T(128)S(1)} %concatenate.34.refs_0_.meta, bf16[16,32,256]{2,1,0:T(8,128)(2,1)S(1)} %copy-done, bf16[16,32,256]{2,1,0:T(8,128)(2,1)S(1)} %collective-permute-done.near, bf16[16,32,256]{2,1,0:T(8,128)(2,1)S(1)} %collective-permute-done.1.far, ...), custom_call_target="tpu_custom_call" | custom-call | tf_op jit(solution)/shard_map/prep/pallas_call | solution.py:161
  32.4 1.8 %side.1 = bf16[1024,256]{1,0:T(8,128)(2,1)S(1)} custom-call(bf16[1024,3072]{1,0:T(8,128)(2,1)S(1)} %load.5.w, bf16[3072,256]{1,0:T(8,128)(2,1)S(1)} %get-tuple-element.7.picked), custom_call_target="tpu_custom_call" | custom-call | tf_op jit(solution)/shard_map/side/pallas_call | solution.py:177
  34.2 0.4 collective-permute-start.9
  34.6 3.3 %collective-permute-start.8 = (bf16[1024,256]{1,0:T(8,128)(2,1)S(1)}, bf16[1024,256]{1,0:T(8,128)(2,1)S(1)}, u32[]{:S(2)}, u32[]{:S(2)}) collective-permute-start(bf16[1024,256]{1,0:T(8,128)(2,1)S(1)} %get-tuple-element.8), channel_id=1, source_target_pairs={{0,7},{1,2},{2,1},{3,4},{4,3},{5,6},{6,5},{7,0},{8,15},{9,10},{10,... | collective-permute-start | bytes 1572872 | tf_op jit(solution)/shard_map/ppermute | solution.py:16
  37.9 3.3 %load.3.w = bf16[1024,3072]{1,0:T(8,128)(2,1)S(1)} custom-call(s32[12]{0:T(128)S(1)} %concatenate.34.refs_0_.meta, bf16[3072,3072]{1,0:T(8,128)(2,1)} %bitcast.14), custom_call_target="tpu_custom_call" | custom-call | flops 4294967296 | bytes 6291456 | tf_op jit(solution)/shard_map/load/pallas_call | solution.py:148
  41.3 1.8 %own.3 = f32[1024,256]{1,0:T(8,128)S(1)} custom-call(bf16[1024,3072]{1,0:T(8,128)(2,1)S(1)} %load.3.w, bf16[3072,256]{1,0:T(8,128)(2,1)S(1)} %get-tuple-element.7.picked), custom_call_target="tpu_custom_call" | custom-call | tf_op jit(solution)/shard_map/own/pallas_call | solution.py:177
  43.1 4.7 %collective-permute-done.9 = bf16[1024,256]{1,0:T(8,128)(2,1)S(1)} collective-permute-done((bf16[1024,256]{1,0:T(8,128)(2,1)S(1)}, bf16[1024,256]{1,0:T(8,128)(2,1)S(1)}, u32[]{:S(2)}, u32[]{:S(2)}) %collective-permute-start.9) | collective-permute-done | bytes 524320 | tf_op jit(solution)/shard_map/ppermute | solution.py:16
  47.8 3.7 %collective-permute-done.8 = bf16[1024,256]{1,0:T(8,128)(2,1)S(1)} collective-permute-done((bf16[1024,256]{1,0:T(8,128)(2,1)S(1)}, bf16[1024,256]{1,0:T(8,128)(2,1)S(1)}, u32[]{:S(2)}, u32[]{:S(2)}) %collective-permute-start.8) | collective-permute-done | bytes 524320 | tf_op jit(solution)/shard_map/ppermute | solution.py:16
  51.4 1.0 %add_convert_fusion = bf16[1024,256]{1,0:T(8,128)(2,1)} fusion(bf16[1024,256]{1,0:T(8,128)(2,1)S(1)} %collective-permute-done.9, f32[1024,256]{1,0:T(8,128)S(1)} %own.3, bf16[1024,256]{1,0:T(8,128)(2,1)S(1)} %collective-permute-done.8), kind=kLoop, calls=%fused_computation | loop fusion | flops 1310720 | bytes 2621440 | tf_op jit(solution)/shard_map/convert_element_type | solution.py:189
  (15 shorter events, 0.1 us)
Async XLA Ops:
  0.0 19.4 %collective-permute-start = (bf16[16,32,256]{2,1,0:T(8,128)(2,1)}, bf16[16,32,256]{2,1,0:T(8,128)(2,1)S(1)}, u32[]{:S(2)}, u32[]{:S(2)}) collective-permute-start(bf16[16,32,256]{2,1,0:T(8,128)(2,1)} %own.2), channel_id=1, source_target_pairs={{0,16},{8,24},{16,0},{24,8},{32,48},{40,56},{48,32},{56,40},{64,80... | collective-permute-start | bytes 786440 | tf_op jit(solution)/shard_map/ppermute | solution.py:16
  2.1 17.3 %collective-permute-start.1 = (bf16[16,32,256]{2,1,0:T(8,128)(2,1)}, bf16[16,32,256]{2,1,0:T(8,128)(2,1)S(1)}, u32[]{:S(2)}, u32[]{:S(2)}) collective-permute-start(bf16[16,32,256]{2,1,0:T(8,128)(2,1)} %own.2), channel_id=1, source_target_pairs={{0,112},{8,120},{16,32},{24,40},{32,16},{40,24},{48,64},{56,72},{6... | collective-permute-start | bytes 786440 | tf_op jit(solution)/shard_map/ppermute | solution.py:16
  6.7 7.3 %collective-permute-start.2 = (bf16[16,256]{1,0:T(8,128)(2,1)S(1)}, bf16[16,256]{1,0:T(8,128)(2,1)S(1)}, u32[]{:S(2)}, u32[]{:S(2)}) collective-permute-start(bf16[16,256]{1,0:T(8,128)(2,1)S(1)} %get-tuple-element.11), channel_id=1, source_target_pairs={{0,7},{1,2},{2,1},{3,4},{4,3},{5,6},{6,5},{7,0},{8,15},{9,10},{10,... | collective-permute-start | bytes 24584 | tf_op jit(solution)/shard_map/ppermute | solution.py:16
  11.9 2.8 %collective-permute-start.3 = (bf16[16,256]{1,0:T(8,128)(2,1)S(1)}, bf16[16,256]{1,0:T(8,128)(2,1)S(1)}, u32[]{:S(2)}, u32[]{:S(2)}) collective-permute-start(bf16[16,256]{1,0:T(8,128)(2,1)S(1)} %get-tuple-element.12), channel_id=1, source_target_pairs={{0,1},{1,0},{2,3},{3,2},{4,5},{5,4},{6,7},{7,6},{8,9},{9,8},{10,11... | collective-permute-start | bytes 24584 | tf_op jit(solution)/shard_map/ppermute | solution.py:16
  12.6 17.2 %collective-permute-start.7 = (bf16[1,32,256]{2,1,0:T(8,128)(2,1)S(1)}, bf16[1,32,256]{2,1,0:T(8,128)(2,1)S(1)}, u32[]{:S(2)}, u32[]{:S(2)}) collective-permute-start(bf16[1,32,256]{2,1,0:T(8,128)(2,1)S(1)} %slice_select_fusion.2), channel_id=1, source_target_pairs={{0,104},{8,32},{16,120},{24,48},{32,8},{40,64},{48,24},{56,80},{64... | collective-permute-start | bytes 49160 | tf_op jit(solution)/shard_map/ppermute | solution.py:16
  14.7 5.8 %collective-permute-start.4 = (bf16[32,256]{1,0:T(8,128)(2,1)S(1)}, bf16[32,256]{1,0:T(8,128)(2,1)S(1)}, u32[]{:S(2)}, u32[]{:S(2)}) collective-permute-start(bf16[32,256]{1,0:T(8,128)(2,1)S(1)} %maximum_select_fusion.own_cols), channel_id=1, source_target_pairs={{0,16},{8,24},{16,0},{24,8},{32,48},{40,56},{48,32},{56,40},{64,80... | collective-permute-start | bytes 49160 | tf_op jit(solution)/shard_map/ppermute | solution.py:16
  15.4 5.2 %collective-permute-start.5 = (bf16[32,256]{1,0:T(8,128)(2,1)S(1)}, bf16[32,256]{1,0:T(8,128)(2,1)S(1)}, u32[]{:S(2)}, u32[]{:S(2)}) collective-permute-start(bf16[32,256]{1,0:T(8,128)(2,1)S(1)} %maximum_select_fusion.own_cols), channel_id=1, source_target_pairs={{0,112},{8,120},{16,32},{24,40},{32,16},{40,24},{48,64},{56,72},{6... | collective-permute-start | bytes 49160 | tf_op jit(solution)/shard_map/ppermute | solution.py:16
  20.7 9.1 %collective-permute-start.6 = (bf16[35,32,256]{2,1,0:T(8,128)(2,1)S(1)}, bf16[35,32,256]{2,1,0:T(8,128)(2,1)S(1)}, u32[]{:S(2)}, u32[]{:S(2)}) collective-permute-start(bf16[35,32,256]{2,1,0:T(8,128)(2,1)S(1)} %fusion.2), channel_id=1, source_target_pairs={{0,8},{8,0},{16,24},{24,16},{32,40},{40,32},{48,56},{56,48},{64,72... | collective-permute-start | bytes 1720328 | tf_op jit(solution)/shard_map/ppermute | solution.py:16
  26.4 3.4 %copy-start = (bf16[16,32,256]{2,1,0:T(8,128)(2,1)S(1)}, bf16[16,32,256]{2,1,0:T(8,128)(2,1)}, u32[]{:S(2)}) copy-start(bf16[16,32,256]{2,1,0:T(8,128)(2,1)} %own.2) | copy-start | bytes 786436
  34.2 13.6 %collective-permute-start.9 = (bf16[1024,256]{1,0:T(8,128)(2,1)S(1)}, bf16[1024,256]{1,0:T(8,128)(2,1)S(1)}, u32[]{:S(2)}, u32[]{:S(2)}) collective-permute-start(bf16[1024,256]{1,0:T(8,128)(2,1)S(1)} %side.1), channel_id=1, source_target_pairs={{0,1},{1,0},{2,3},{3,2},{4,5},{5,4},{6,7},{7,6},{8,9},{9,8},{10,11... | collective-permute-start | bytes 1572872 | tf_op jit(solution)/shard_map/ppermute | solution.py:16
  34.6 16.8 %collective-permute-start.8 = (bf16[1024,256]{1,0:T(8,128)(2,1)S(1)}, bf16[1024,256]{1,0:T(8,128)(2,1)S(1)}, u32[]{:S(2)}, u32[]{:S(2)}) collective-permute-start(bf16[1024,256]{1,0:T(8,128)(2,1)S(1)} %get-tuple-element.8), channel_id=1, source_target_pairs={{0,7},{1,2},{2,1},{3,4},{4,3},{5,6},{6,5},{7,0},{8,15},{9,10},{10,... | collective-permute-start | bytes 1572872 | tf_op jit(solution)/shard_map/ppermute | solution.py:16

commit v2 on v1

v2 whole, which is shorter than its diff:
```python
import jax
import jax.numpy as jnp
from jax import lax
from jax.experimental import pallas as pl
from jax.experimental.pallas import tpu as pltpu
from jax.sharding import PartitionSpec as P

STRIP_ROWS = 4
SLOTS = 8
REACH = 2
CHUNKS = 4
BF16 = jnp.bfloat16
F32 = jnp.float32


def swap(block, axis, partner):
    return lax.ppermute(block, axis, [(i, partner(i)) for i in range(lax.axis_size(axis))])


def near_chip(i):
    return i ^ 2


def inside(to, spare, count=16):
    return to if 0 <= to < count else spare


def far_chip(i):
    return inside(i + 2 if (i // 2) % 2 else i - 2, i ^ 1)


def edges_body(field, tile, far_edge, near_edge, edge_row):
    core, parity = lax.axis_index("lat") % 2, lax.axis_index("lon") % 2
    tile[...] = field[...]
    last = field.shape[1] - 1
    for i in range(field.shape[0]):
        west, east = field[i, :1], field[i, last:]
        far_edge[i : i + 1] = jnp.where(parity == 0, west, east)
        near_edge[i : i + 1] = jnp.where(parity == 0, east, west)
    edge_row[...] = jnp.where(core == 1, field[-1:], field[:1])


def load_body(w, block, sem, *, far):
    parity = lax.axis_index("lon") % 2
    size = block.shape[0]
    start = jnp.where(parity == (0 if far else 1), 0, 2 * size)
    copy = pltpu.make_async_copy(w.at[pl.ds(start, size)], block, sem)
    copy.start()
    copy.wait()


def prep_body(ids, counts, own, near, far, mate, beyond, own_cols, near_cols, far_cols, w, picked, out, rows, west, east):
    rows_per = own.shape[0]
    band = lax.axis_index("lat")
    bands = lax.axis_size("lat")
    core, odd = band % 2, (band // 2) % 2
    slot_of_near = jnp.where(odd == 1, 0, 2 * REACH)
    slot_of_far = 2 * REACH - slot_of_near
    slot_of_hop = jnp.where(core == 0, REACH - 1, REACH + 1)
    slot_of_mate = 2 * REACH - slot_of_hop

    def place(slot, tile, cols):
        rows[pl.ds(1 + slot * rows_per, rows_per)] = tile
        for i in range(rows_per):
            west[slot * rows_per + i] = cols[i : i + 1]
            east[slot * rows_per + i] = cols[rows_per + i : rows_per + i + 1]

    place(REACH, own[...], own_cols[...].astype(F32))
    place(slot_of_near, near[...], near_cols[...].astype(F32))
    place(slot_of_far, far[...], far_cols[...].astype(F32))
    place(slot_of_hop, mate[:rows_per], mate[2 * rows_per + 1].astype(F32))
    place(slot_of_mate, mate[rows_per : 2 * rows_per], mate[2 * rows_per + 2].astype(F32))
    last = (2 * REACH + 1) * rows_per + 1
    rows[jnp.where(core == 0, 0, last)] = beyond[0]
    rows[jnp.where(core == 0, last, 0)] = mate[2 * rows_per]

    @pl.when(band <= REACH)
    def _():
        edge = rows_per * (REACH - band)
        rows[edge] = rows[edge + 1]

    @pl.when(band >= bands - 1 - REACH)
    def _():
        edge = rows_per * (bands + REACH - band)
        rows[edge + 1] = rows[edge]

    lon, chan = own.shape[1], own.shape[2]
    cells = STRIP_ROWS * lon
    first_strip = (band - REACH) * (rows_per // STRIP_ROWS)
    place_in_row = lax.broadcasted_iota(jnp.int32, (STRIP_ROWS, lon, chan), 1)
    for k in range(SLOTS):
        base = STRIP_ROWS * (ids[0, k] - first_strip)
        block = rows[pl.ds(base, STRIP_ROWS + 2)].astype(F32)
        centre = block[1:-1]
        north = (block[2:] - block[:-2]) * 0.5
        flat = centre.reshape(cells, chan)
        before = pltpu.roll(flat, 1, axis=0).reshape(centre.shape)
        after = pltpu.roll(flat, cells - 1, axis=0).reshape(centre.shape)
        before = jnp.where(place_in_row == 0, west[pl.ds(base, STRIP_ROWS)], before)
        after = jnp.where(place_in_row == lon - 1, east[pl.ds(base, STRIP_ROWS)], after)
        eastward = (after - before) * 0.5
        live = k < counts[0]
        for c, part in enumerate((centre, eastward, north)):
            start = (3 * k + c) * cells
            part = jnp.where(live, part.reshape(cells, chan), 0.0)
            picked[start : start + cells] = part.astype(BF16)
    out[...] = jnp.dot(w[...], picked[...], preferred_element_type=F32).astype(BF16)


def side_body(w, picked, out):
    out[...] = jnp.dot(w[...], picked[...], preferred_element_type=F32).astype(BF16)


def own_body(w, picked, out, held, sems):
    size = out.shape[0]
    part = size // CHUNKS
    copies = [
        pltpu.make_async_copy(
            w.at[pl.ds(size + part * c, part)], held.at[pl.ds(part * c, part)], sems.at[c]
        )
        for c in range(CHUNKS)
    ]
    for copy in copies:
        copy.start()
    for c, copy in enumerate(copies):
        copy.wait()
        here = slice(part * c, part * (c + 1))
        out[here] = jnp.dot(held[here], picked[...], preferred_element_type=F32)


def remap(field, weights, strip_ids, counts):
    band, sector = lax.axis_index("lat"), lax.axis_index("lon")
    core, odd, parity = band % 2, (band // 2) % 2, sector % 2
    rows_per, lon, chan = field.shape
    near_lon = lambda i: i ^ 1
    far_lon = lambda i: (i + 1) % 8 if i % 2 else (i - 1) % 8
    vmem = pl.BlockSpec(memory_space=pltpu.VMEM)
    smem = pl.BlockSpec(memory_space=pltpu.SMEM)
    hbm = pl.BlockSpec(memory_space=pltpu.HBM)
    held = lambda x: pltpu.with_memory_space_constraint(x, pltpu.VMEM)
    small = pltpu.CompilerParams(vmem_limit_bytes=2 << 20)

    tile, far_edge, near_edge, edge_row = pl.pallas_call(
        edges_body,
        in_specs=[vmem],
        out_specs=[vmem] * 4,
        out_shape=[
            pltpu.VMEM(field.shape, BF16),
            pltpu.VMEM((rows_per, chan), BF16),
            pltpu.VMEM((rows_per, chan), BF16),
            pltpu.VMEM((1, lon, chan), BF16),
        ],
        compiler_params=small,
        name="edges",
    )(field)
    far = swap(tile, "lat", far_chip)
    near = swap(tile, "lat", near_chip)
    from_far = swap(far_edge, "lon", far_lon)
    from_near = swap(near_edge, "lon", near_lon)
    beyond = swap(edge_row, "lat", lambda i: inside(i + 3 if i % 2 else i - 3, i ^ 2))
    cols = jnp.where(
        parity == 0, jnp.concatenate([from_far, from_near]), jnp.concatenate([from_near, from_far])
    )
    far_cols = swap(cols, "lat", far_chip)
    near_cols = swap(cols, "lat", near_chip)

    w = pltpu.with_memory_space_constraint(weights[0, 0], pltpu.HBM)
    size = w.shape[0] // 3
    width = w.shape[1]

    def load(far):
        return pl.pallas_call(
            lambda *refs: load_body(*refs, far=far),
            in_specs=[hbm],
            out_specs=vmem,
            out_shape=pltpu.VMEM((size, width), BF16),
            scratch_shapes=[pltpu.SemaphoreType.DMA],
            compiler_params=small,
        )(w)

    w_far, w_near = load(True), load(False)

    pick_near = core == odd
    other_rows = jnp.where(
        core == 0,
        jnp.where(pick_near, far[-1:], near[-1:]),
        jnp.where(pick_near, far[:1], near[:1]),
    )
    message = jnp.concatenate(
        [
            jnp.where(pick_near, near, far),
            tile,
            other_rows,
            jnp.where(pick_near, near_cols, far_cols)[None],
            cols[None],
        ]
    )
    mate = swap(message, "lat", lambda i: i ^ 1)

    halo = (2 * REACH + 1) * rows_per
    picked, to_far = pl.pallas_call(
        prep_body,
        in_specs=[smem, smem] + [vmem] * 9,
        out_specs=[vmem, vmem],
        out_shape=[pltpu.VMEM((width, chan), BF16), pltpu.VMEM((size, chan), BF16)],
        scratch_shapes=[
            pltpu.VMEM((halo + 2, lon, chan), BF16),
            pltpu.VMEM((halo, 1, chan), F32),
            pltpu.VMEM((halo, 1, chan), F32),
        ],
        compiler_params=pltpu.CompilerParams(vmem_limit_bytes=16 << 20),
        name="prep",
    )(strip_ids, counts, held(tile), near, far, mate, beyond, cols, near_cols, far_cols, held(w_far))
    picked = held(picked)
    got_far = swap(to_far, "lon", far_lon)
    to_near = pl.pallas_call(
        side_body,
        in_specs=[vmem, vmem],
        out_specs=vmem,
        out_shape=pltpu.VMEM((size, chan), BF16),
        compiler_params=pltpu.CompilerParams(vmem_limit_bytes=16 << 20),
        name="side",
    )(held(w_near), picked)
    got_near = swap(to_near, "lon", near_lon)
    own = pl.pallas_call(
        own_body,
        in_specs=[hbm, vmem],
        out_specs=vmem,
        out_shape=pltpu.VMEM((size, chan), F32),
        scratch_shapes=[pltpu.VMEM((size, width), BF16), pltpu.SemaphoreType.DMA((CHUNKS,))],
        compiler_params=pltpu.CompilerParams(vmem_limit_bytes=16 << 20),
        name="own",
    )(w, picked)
    return (own + got_far.astype(F32) + got_near.astype(F32)).astype(BF16)


def solution(mesh):
    placed = (P("lat", "lon", None), P("lat", "lon", None, None), P("lat", None), P("lat"))
    return jax.shard_map(
        remap, mesh=mesh, in_specs=placed, out_specs=P(("lat", "lon"), None), check_vma=False
    )
```

time: 52.8 us -> 51.4 us (0.973)
  waiting for transfers between devices: 9.23 us -> 11.1 us
  local copies, waits for them, and re-layouts: 2.61 us -> 0.98 us
  Pallas kernels: 16.2 us -> 15.3 us
  other arithmetic: 1.85 us -> 1.06 us
    ppermute x10, waiting for transfers between devices: 9.23 us -> 11.1 us  [swap(): lax.ppermute(block, axis, [(i, partner(i)) for i in range(lax.axis_size(a...]
    slice x1 -> x0, local copies, waits for them, and re-layouts: 0.9 us -> none  [body(): west_edge, east_edge = (field[:, 0], field[:, -1])]
    pallas_call x6, Pallas kernels: 16.2 us -> 15.3 us  [the longest x2 5.6 us: load(): pl.pallas_call(lambda *refs: load_body(*refs, far=far), in_specs=[hbm], o...]
    select_n x3 -> x1, other arithmetic: 0.75 us -> 0.01 us  [remap(): jnp.where(parity == 0, jnp.concatenate([from_far, from_near]), jnp.concat...]
    concatenate x1 -> x0, local copies, waits for them, and re-layouts: 0.74 us -> none  [body(): jnp.concatenate([jnp.stack([band, parity, bands]).astype(jnp.int32), coun...]
  transfers between devices with their start and end apart: 10 -> 10, of which waited for: 4 -> 5; matrix products, arithmetic and copies ran while one was open for 7% -> 0% of each run, Pallas kernels for 23% -> 21%
where the time goes in v2:
time: 51.4 us; the launch traced here: 51.2 us
  starting transfers between devices  22 us (43%)
  Pallas kernels  15.3 us (30%)
  waiting for transfers between devices  11.1 us (22%)
  other arithmetic  1.06 us (2%)
  local copies, waits for them, and re-layouts  0.98 us (2%)
  between operations  0.77 us (1%)
    ppermute x10, starting transfers between devices, swap(): lax.ppermute(block, axis, [(i, partner(i)) for i in range(lax.axis_size(a...  22 us
    ppermute x10, waiting for transfers between devices, swap(): lax.ppermute(block, axis, [(i, partner(i)) for i in range(lax.axis_size(a...  11.1 us
    pallas_call x2, Pallas kernels, load(): pl.pallas_call(lambda *refs: load_body(*refs, far=far), in_specs=[hbm], o...  5.6 us
    pallas_call x1, Pallas kernels, remap(): pl.pallas_call(own_body, in_specs=[hbm, vmem], out_specs=vmem, out_shape=...  5.29 us
    pallas_call x1, Pallas kernels, remap(): pl.pallas_call(prep_body, in_specs=[smem, smem] + [vmem] * 9, out_specs=[...  2.58 us
    pallas_call x1, Pallas kernels, remap(): pl.pallas_call(side_body, in_specs=[vmem, vmem], out_specs=vmem, out_shap...  1.79 us
  transfers between devices with their start and end apart: 10, of which 5 were waited for; matrix products, arithmetic and copies ran while one was open for 0% of the time, Pallas kernels for 21%

profile of v2, /device:TPU:1, one launch (start us, length us, event | category | flops | bytes accessed | tf_op | source)
XLA Modules:
  0.0 51.2 jit_solution(4170424578191957235)
XLA Ops:
  0.0 0.9 %copy-done = bf16[16,32,256]{2,1,0:T(8,128)(2,1)S(1)} copy-done((bf16[16,32,256]{2,1,0:T(8,128)(2,1)S(1)}, bf16[16,32,256]{2,1,0:T(8,128)(2,1)}, u32[]{:S(2)}) %copy-start) | copy-done | bytes 262168
  1.0 0.1 edges.1
  1.0 2.2 %collective-permute-start = (bf16[16,32,256]{2,1,0:T(8,128)(2,1)S(1)}, bf16[16,32,256]{2,1,0:T(8,128)(2,1)S(1)}, u32[]{:S(2)}, u32[]{:S(2)}) collective-permute-start(bf16[16,32,256]{2,1,0:T(8,128)(2,1)S(1)} %get-tuple-element.11.own), channel_id=1, source_target_pairs={{0,16},{8,24},{16,0},{24,8},{32,48},{40,56},{48,32},{56,40},{64,80... | collective-permute-start | bytes 786440 | tf_op jit(solution)/shard_map/ppermute | solution.py:17
  3.2 1.0 %collective-permute-start.1 = (bf16[16,32,256]{2,1,0:T(8,128)(2,1)S(1)}, bf16[16,32,256]{2,1,0:T(8,128)(2,1)S(1)}, u32[]{:S(2)}, u32[]{:S(2)}) collective-permute-start(bf16[16,32,256]{2,1,0:T(8,128)(2,1)S(1)} %get-tuple-element.11.own), channel_id=1, source_target_pairs={{0,8},{8,0},{16,32},{24,40},{32,16},{40,24},{48,64},{56,72},{64,48... | collective-permute-start | bytes 786440 | tf_op jit(solution)/shard_map/ppermute | solution.py:17
  4.2 4.8 %collective-permute-start.2 = (bf16[16,256]{1,0:T(8,128)(2,1)S(1)}, bf16[16,256]{1,0:T(8,128)(2,1)S(1)}, u32[]{:S(2)}, u32[]{:S(2)}) collective-permute-start(bf16[16,256]{1,0:T(8,128)(2,1)S(1)} %get-tuple-element.12), channel_id=1, source_target_pairs={{0,7},{1,2},{2,1},{3,4},{4,3},{5,6},{6,5},{7,0},{8,15},{9,10},{10,... | collective-permute-start | bytes 24584 | tf_op jit(solution)/shard_map/ppermute | solution.py:17
  9.0 1.4 %collective-permute-done.2 = bf16[16,256]{1,0:T(8,128)(2,1)S(1)} collective-permute-done((bf16[16,256]{1,0:T(8,128)(2,1)S(1)}, bf16[16,256]{1,0:T(8,128)(2,1)S(1)}, u32[]{:S(2)}, u32[]{:S(2)}) %collective-permute-start.2) | collective-permute-done | bytes 8224 | tf_op jit(solution)/shard_map/ppermute | solution.py:17
  10.4 1.1 %collective-permute-done.3 = bf16[16,256]{1,0:T(8,128)(2,1)S(1)} collective-permute-done((bf16[16,256]{1,0:T(8,128)(2,1)S(1)}, bf16[16,256]{1,0:T(8,128)(2,1)S(1)}, u32[]{:S(2)}, u32[]{:S(2)}) %collective-permute-start.3) | collective-permute-done | bytes 8224 | tf_op jit(solution)/shard_map/ppermute | solution.py:17
  11.5 1.6 %collective-permute-start.4 = (bf16[32,256]{1,0:T(8,128)(2,1)S(1)}, bf16[32,256]{1,0:T(8,128)(2,1)S(1)}, u32[]{:S(2)}, u32[]{:S(2)}) collective-permute-start(bf16[32,256]{1,0:T(8,128)(2,1)S(1)} %maximum_select_fusion.own_cols), channel_id=1, source_target_pairs={{0,16},{8,24},{16,0},{24,8},{32,48},{40,56},{48,32},{56,40},{64,80... | collective-permute-start | bytes 49160 | tf_op jit(solution)/shard_map/ppermute | solution.py:17
  13.0 2.6 %collective-permute-start.5 = (bf16[32,256]{1,0:T(8,128)(2,1)S(1)}, bf16[32,256]{1,0:T(8,128)(2,1)S(1)}, u32[]{:S(2)}, u32[]{:S(2)}) collective-permute-start(bf16[32,256]{1,0:T(8,128)(2,1)S(1)} %maximum_select_fusion.own_cols), channel_id=1, source_target_pairs={{0,8},{8,0},{16,32},{24,40},{32,16},{40,24},{48,64},{56,72},{64,48... | collective-permute-start | bytes 49160 | tf_op jit(solution)/shard_map/ppermute | solution.py:17
  15.7 0.1 select_dynamic-update-slice_fusion
  15.8 0.7 %collective-permute-done.5.far_cols = bf16[32,256]{1,0:T(8,128)(2,1)S(1)} collective-permute-done((bf16[32,256]{1,0:T(8,128)(2,1)S(1)}, bf16[32,256]{1,0:T(8,128)(2,1)S(1)}, u32[]{:S(2)}, u32[]{:S(2)}) %collective-permute-start.5) | collective-permute-done | bytes 16416 | tf_op jit(solution)/shard_map/ppermute | solution.py:17
  16.5 1.0 %collective-permute-start.6 = (bf16[35,32,256]{2,1,0:T(8,128)(2,1)S(1)}, bf16[35,32,256]{2,1,0:T(8,128)(2,1)S(1)}, u32[]{:S(2)}, u32[]{:S(2)}) collective-permute-start(bf16[35,32,256]{2,1,0:T(8,128)(2,1)S(1)} %fusion.2), channel_id=1, source_target_pairs={{0,8},{8,0},{16,24},{24,16},{32,40},{40,32},{48,56},{56,48},{64,72... | collective-permute-start | bytes 1720328 | tf_op jit(solution)/shard_map/ppermute | solution.py:17
  17.5 4.5 %collective-permute-start.7 = (bf16[1,32,256]{2,1,0:T(8,128)(2,1)S(1)}, bf16[1,32,256]{2,1,0:T(8,128)(2,1)S(1)}, u32[]{:S(2)}, u32[]{:S(2)}) collective-permute-start(bf16[1,32,256]{2,1,0:T(8,128)(2,1)S(1)} %get-tuple-element.14), channel_id=1, source_target_pairs={{0,16},{8,32},{16,0},{24,48},{32,8},{40,64},{48,24},{56,80},{64,40... | collective-permute-start | bytes 49160 | tf_op jit(solution)/shard_map/ppermute | solution.py:17
  22.0 2.8 %shard_map.46.w = bf16[1024,3072]{1,0:T(8,128)(2,1)S(1)} custom-call(bf16[3072,3072]{1,0:T(8,128)(2,1)} %bitcast.5), custom_call_target="tpu_custom_call" | custom-call | tf_op jit(solution)/shard_map/pallas_call | solution.py:172
  24.8 0.0 copy-start.1
  24.9 2.8 %shard_map.47.w = bf16[1024,3072]{1,0:T(8,128)(2,1)S(1)} custom-call(bf16[3072,3072]{1,0:T(8,128)(2,1)} %bitcast.6), custom_call_target="tpu_custom_call" | custom-call | tf_op jit(solution)/shard_map/pallas_call | solution.py:172
  28.3 2.6 %prep.1 = (bf16[3072,256]{1,0:T(8,128)(2,1)S(1)}, bf16[1024,256]{1,0:T(8,128)(2,1)S(1)}) custom-call(s32[1,8]{1,0:T(1,128)S(1)} %copy-done.1, s32[1]{0:T(128)S(6)} %copy.9.counts, bf16[16,32,256]{2,1,0:T(8,128)(2,1)S(1)} %get-tuple-element.11.own, bf16[16,32,256]{2,1,0:T(8,128)(2,1)S(1)} %collective-permute-done.near, ...), custom_call_target="tpu_custom_call" | custom-call | tf_op jit(solution)/shard_map/prep/pallas_call | solution.py:201
  30.9 1.8 %side.1 = bf16[1024,256]{1,0:T(8,128)(2,1)S(1)} custom-call(bf16[1024,3072]{1,0:T(8,128)(2,1)S(1)} %shard_map.47.w, bf16[3072,256]{1,0:T(8,128)(2,1)S(1)} %get-tuple-element.15.picked), custom_call_target="tpu_custom_call" | custom-call | tf_op jit(solution)/shard_map/side/pallas_call | solution.py:216
  32.7 0.1 collective-permute-start.9
  32.8 4.2 %collective-permute-start.8 = (bf16[1024,256]{1,0:T(8,128)(2,1)S(1)}, bf16[1024,256]{1,0:T(8,128)(2,1)S(1)}, u32[]{:S(2)}, u32[]{:S(2)}) collective-permute-start(bf16[1024,256]{1,0:T(8,128)(2,1)S(1)} %get-tuple-element.16), channel_id=1, source_target_pairs={{0,7},{1,2},{2,1},{3,4},{4,3},{5,6},{6,5},{7,0},{8,15},{9,10},{10,... | collective-permute-start | bytes 1572872 | tf_op jit(solution)/shard_map/ppermute | solution.py:17
  37.0 5.3 %own.1 = f32[1024,256]{1,0:T(8,128)S(1)} custom-call(bf16[3072,3072]{1,0:T(8,128)(2,1)} %bitcast.7, bf16[3072,256]{1,0:T(8,128)(2,1)S(1)} %get-tuple-element.15.picked), custom_call_target="tpu_custom_call" | custom-call | tf_op jit(solution)/shard_map/own/pallas_call | solution.py:225
  42.3 4.0 %collective-permute-done.9 = bf16[1024,256]{1,0:T(8,128)(2,1)S(1)} collective-permute-done((bf16[1024,256]{1,0:T(8,128)(2,1)S(1)}, bf16[1024,256]{1,0:T(8,128)(2,1)S(1)}, u32[]{:S(2)}, u32[]{:S(2)}) %collective-permute-start.9) | collective-permute-done | bytes 524320 | tf_op jit(solution)/shard_map/ppermute | solution.py:17
  46.3 3.9 %collective-permute-done.8 = bf16[1024,256]{1,0:T(8,128)(2,1)S(1)} collective-permute-done((bf16[1024,256]{1,0:T(8,128)(2,1)S(1)}, bf16[1024,256]{1,0:T(8,128)(2,1)S(1)}, u32[]{:S(2)}, u32[]{:S(2)}) %collective-permute-start.8) | collective-permute-done | bytes 524320 | tf_op jit(solution)/shard_map/ppermute | solution.py:17
  50.2 0.9 %add_convert_fusion = bf16[1024,256]{1,0:T(8,128)(2,1)} fusion(bf16[1024,256]{1,0:T(8,128)(2,1)S(1)} %collective-permute-done.9, f32[1024,256]{1,0:T(8,128)S(1)} %own.1, bf16[1024,256]{1,0:T(8,128)(2,1)S(1)} %collective-permute-done.8), kind=kLoop, calls=%fused_computation | loop fusion | flops 1310720 | bytes 2621440 | tf_op jit(solution)/shard_map/convert_element_type | solution.py:234
  (13 shorter events, 0.1 us)
Async XLA Ops:
  0.0 0.9 %copy-start = (bf16[16,32,256]{2,1,0:T(8,128)(2,1)S(1)}, bf16[16,32,256]{2,1,0:T(8,128)(2,1)}, u32[]{:S(2)}) copy-start(bf16[16,32,256]{2,1,0:T(8,128)(2,1)} %field.1) | copy-start | bytes 786436
  1.0 14.7 %collective-permute-start = (bf16[16,32,256]{2,1,0:T(8,128)(2,1)S(1)}, bf16[16,32,256]{2,1,0:T(8,128)(2,1)S(1)}, u32[]{:S(2)}, u32[]{:S(2)}) collective-permute-start(bf16[16,32,256]{2,1,0:T(8,128)(2,1)S(1)} %get-tuple-element.11.own), channel_id=1, source_target_pairs={{0,16},{8,24},{16,0},{24,8},{32,48},{40,56},{48,32},{56,40},{64,80... | collective-permute-start | bytes 786440 | tf_op jit(solution)/shard_map/ppermute | solution.py:17
  3.2 12.5 %collective-permute-start.1 = (bf16[16,32,256]{2,1,0:T(8,128)(2,1)S(1)}, bf16[16,32,256]{2,1,0:T(8,128)(2,1)S(1)}, u32[]{:S(2)}, u32[]{:S(2)}) collective-permute-start(bf16[16,32,256]{2,1,0:T(8,128)(2,1)S(1)} %get-tuple-element.11.own), channel_id=1, source_target_pairs={{0,8},{8,0},{16,32},{24,40},{32,16},{40,24},{48,64},{56,72},{64,48... | collective-permute-start | bytes 786440 | tf_op jit(solution)/shard_map/ppermute | solution.py:17
  4.2 6.2 %collective-permute-start.2 = (bf16[16,256]{1,0:T(8,128)(2,1)S(1)}, bf16[16,256]{1,0:T(8,128)(2,1)S(1)}, u32[]{:S(2)}, u32[]{:S(2)}) collective-permute-start(bf16[16,256]{1,0:T(8,128)(2,1)S(1)} %get-tuple-element.12), channel_id=1, source_target_pairs={{0,7},{1,2},{2,1},{3,4},{4,3},{5,6},{6,5},{7,0},{8,15},{9,10},{10,... | collective-permute-start | bytes 24584 | tf_op jit(solution)/shard_map/ppermute | solution.py:17
  9.0 2.5 %collective-permute-start.3 = (bf16[16,256]{1,0:T(8,128)(2,1)S(1)}, bf16[16,256]{1,0:T(8,128)(2,1)S(1)}, u32[]{:S(2)}, u32[]{:S(2)}) collective-permute-start(bf16[16,256]{1,0:T(8,128)(2,1)S(1)} %get-tuple-element.13), channel_id=1, source_target_pairs={{0,1},{1,0},{2,3},{3,2},{4,5},{5,4},{6,7},{7,6},{8,9},{9,8},{10,11... | collective-permute-start | bytes 24584 | tf_op jit(solution)/shard_map/ppermute | solution.py:17
  11.5 4.4 %collective-permute-start.4 = (bf16[32,256]{1,0:T(8,128)(2,1)S(1)}, bf16[32,256]{1,0:T(8,128)(2,1)S(1)}, u32[]{:S(2)}, u32[]{:S(2)}) collective-permute-start(bf16[32,256]{1,0:T(8,128)(2,1)S(1)} %maximum_select_fusion.own_cols), channel_id=1, source_target_pairs={{0,16},{8,24},{16,0},{24,8},{32,48},{40,56},{48,32},{56,40},{64,80... | collective-permute-start | bytes 49160 | tf_op jit(solution)/shard_map/ppermute | solution.py:17
  13.0 3.5 %collective-permute-start.5 = (bf16[32,256]{1,0:T(8,128)(2,1)S(1)}, bf16[32,256]{1,0:T(8,128)(2,1)S(1)}, u32[]{:S(2)}, u32[]{:S(2)}) collective-permute-start(bf16[32,256]{1,0:T(8,128)(2,1)S(1)} %maximum_select_fusion.own_cols), channel_id=1, source_target_pairs={{0,8},{8,0},{16,32},{24,40},{32,16},{40,24},{48,64},{56,72},{64,48... | collective-permute-start | bytes 49160 | tf_op jit(solution)/shard_map/ppermute | solution.py:17
  16.5 11.8 %collective-permute-start.6 = (bf16[35,32,256]{2,1,0:T(8,128)(2,1)S(1)}, bf16[35,32,256]{2,1,0:T(8,128)(2,1)S(1)}, u32[]{:S(2)}, u32[]{:S(2)}) collective-permute-start(bf16[35,32,256]{2,1,0:T(8,128)(2,1)S(1)} %fusion.2), channel_id=1, source_target_pairs={{0,8},{8,0},{16,24},{24,16},{32,40},{40,32},{48,56},{56,48},{64,72... | collective-permute-start | bytes 1720328 | tf_op jit(solution)/shard_map/ppermute | solution.py:17
  17.5 10.8 %collective-permute-start.7 = (bf16[1,32,256]{2,1,0:T(8,128)(2,1)S(1)}, bf16[1,32,256]{2,1,0:T(8,128)(2,1)S(1)}, u32[]{:S(2)}, u32[]{:S(2)}) collective-permute-start(bf16[1,32,256]{2,1,0:T(8,128)(2,1)S(1)} %get-tuple-element.14), channel_id=1, source_target_pairs={{0,16},{8,32},{16,0},{24,48},{32,8},{40,64},{48,24},{56,80},{64,40... | collective-permute-start | bytes 49160 | tf_op jit(solution)/shard_map/ppermute | solution.py:17
  24.8 3.5 %copy-start.1 = (s32[1,8]{1,0:T(1,128)S(1)}, s32[1,8]{1,0:T(1,128)}, u32[]{:S(2)}) copy-start(s32[1,8]{1,0:T(1,128)} %ids.1) | copy-start | bytes 100
  32.7 13.6 %collective-permute-start.9 = (bf16[1024,256]{1,0:T(8,128)(2,1)S(1)}, bf16[1024,256]{1,0:T(8,128)(2,1)S(1)}, u32[]{:S(2)}, u32[]{:S(2)}) collective-permute-start(bf16[1024,256]{1,0:T(8,128)(2,1)S(1)} %side.1), channel_id=1, source_target_pairs={{0,1},{1,0},{2,3},{3,2},{4,5},{5,4},{6,7},{7,6},{8,9},{9,8},{10,11... | collective-permute-start | bytes 1572872 | tf_op jit(solution)/shard_map/ppermute | solution.py:17
  32.8 17.4 %collective-permute-start.8 = (bf16[1024,256]{1,0:T(8,128)(2,1)S(1)}, bf16[1024,256]{1,0:T(8,128)(2,1)S(1)}, u32[]{:S(2)}, u32[]{:S(2)}) collective-permute-start(bf16[1024,256]{1,0:T(8,128)(2,1)S(1)} %get-tuple-element.16), channel_id=1, source_target_pairs={{0,7},{1,2},{2,1},{3,4},{4,3},{5,6},{6,5},{7,0},{8,15},{9,10},{10,... | collective-permute-start | bytes 1572872 | tf_op jit(solution)/shard_map/ppermute | solution.py:17

commit v3 on v2

--- a/solution.py
+++ b/solution.py
@@ -40,16 +40,35 @@
     edge_row[...] = jnp.where(core == 1, field[-1:], field[:1])
 
 
-def load_body(w, block, sem, *, far):
-    parity = lax.axis_index("lon") % 2
-    size = block.shape[0]
-    start = jnp.where(parity == (0 if far else 1), 0, 2 * size)
-    copy = pltpu.make_async_copy(w.at[pl.ds(start, size)], block, sem)
+def rows_of(w, far, first, count):
+    even = lax.axis_index("lon") % 2 == 0
+    top = jnp.where(even, 0, 2 * w.shape[0] // 3) if far else jnp.where(even, 2 * w.shape[0] // 3, 0)
+    return w.at[pl.ds(top + first, count)]
+
+
+def load_body(w, far, sem):
+    half = far.shape[0] // 2
+    copy = pltpu.make_async_copy(rows_of(w, True, 0, half), far.at[pl.ds(0, half)], sem)
     copy.start()
     copy.wait()
 
 
-def prep_body(ids, counts, own, near, far, mate, beyond, own_cols, near_cols, far_cols, w, picked, out, rows, west, east):
+def more_body(w, _, far, near, sems):
+    half = far.shape[0] // 2
+    copies = (
+        pltpu.make_async_copy(rows_of(w, True, half, half), far.at[pl.ds(half, half)], sems.at[0]),
+        pltpu.make_async_copy(rows_of(w, False, 0, half), near.at[pl.ds(0, half)], sems.at[1]),
+    )
+    for copy in copies:
+        copy.start()
+    for copy in copies:
+        copy.wait()
+
+
+def prep_body(ids, counts, own, near, far, mate, beyond, own_cols, near_cols, far_cols, w, w_all, _, picked, out, w_near, rows, west, east, sem):
+    half = w_near.shape[0] // 2
+    coming = pltpu.make_async_copy(rows_of(w_all, False, half, half), w_near.at[pl.ds(half, half)], sem)
+    coming.start()
     rows_per = own.shape[0]
     band = lax.axis_index("lat")
     bands = lax.axis_size("lat")
@@ -105,6 +124,7 @@
             part = jnp.where(live, part.reshape(cells, chan), 0.0)
             picked[start : start + cells] = part.astype(BF16)
     out[...] = jnp.dot(w[...], picked[...], preferred_element_type=F32).astype(BF16)
+    coming.wait()
 
 
 def side_body(w, picked, out):
@@ -168,17 +188,26 @@
     size = w.shape[0] // 3
     width = w.shape[1]
 
-    def load(far):
-        return pl.pallas_call(
-            lambda *refs: load_body(*refs, far=far),
-            in_specs=[hbm],
-            out_specs=vmem,
-            out_shape=pltpu.VMEM((size, width), BF16),
-            scratch_shapes=[pltpu.SemaphoreType.DMA],
-            compiler_params=small,
-        )(w)
-
-    w_far, w_near = load(True), load(False)
+    block = pltpu.VMEM((size, width), BF16)
+    w_far = pl.pallas_call(
+        load_body,
+        in_specs=[hbm],
+        out_specs=vmem,
+        out_shape=block,
+        scratch_shapes=[pltpu.SemaphoreType.DMA],
+        compiler_params=small,
+        name="load_far",
+    )(w)
+    w_far, w_near = pl.pallas_call(
+        more_body,
+        in_specs=[hbm, vmem],
+        out_specs=[vmem, vmem],
+        out_shape=[block, block],
+        scratch_shapes=[pltpu.SemaphoreType.DMA((2,))],
+        input_output_aliases={1: 0},
+        compiler_params=small,
+        name="load_more",
+    )(w, held(w_far))
 
     pick_near = core == odd
     other_rows = jnp.where(
@@ -198,19 +227,25 @@
     mate = swap(message, "lat", lambda i: i ^ 1)
 
     halo = (2 * REACH + 1) * rows_per
-    picked, to_far = pl.pallas_call(
+    picked, to_far, w_near = pl.pallas_call(
         prep_body,
-        in_specs=[smem, smem] + [vmem] * 9,
-        out_specs=[vmem, vmem],
-        out_shape=[pltpu.VMEM((width, chan), BF16), pltpu.VMEM((size, chan), BF16)],
+        in_specs=[smem, smem] + [vmem] * 9 + [hbm, vmem],
+        input_output_aliases={12: 2},
+        out_specs=[vmem] * 3,
+        out_shape=[
+            pltpu.VMEM((width, chan), BF16),
+            pltpu.VMEM((size, chan), BF16),
+            pltpu.VMEM((size, width), BF16),
+        ],
         scratch_shapes=[
             pltpu.VMEM((halo + 2, lon, chan), BF16),
             pltpu.VMEM((halo, 1, chan), F32),
             pltpu.VMEM((halo, 1, chan), F32),
+            pltpu.SemaphoreType.DMA,
         ],
         compiler_params=pltpu.CompilerParams(vmem_limit_bytes=16 << 20),
         name="prep",
-    )(strip_ids, counts, held(tile), near, far, mate, beyond, cols, near_cols, far_cols, held(w_far))
+    )(strip_ids, counts, held(tile), near, far, mate, beyond, cols, near_cols, far_cols, held(w_far), w, held(w_near))
     picked = held(picked)
     got_far = swap(to_far, "lon", far_lon)
     to_near = pl.pallas_call(

time: 51.4 us -> 49.5 us (0.963)
  the two profiles are of different devices: /device:TPU:1 before, /device:TPU:0 now
where the time goes in v3:
time: 49.5 us; the launch traced here: 49.4 us
  starting transfers between devices  18.3 us (37%)
  Pallas kernels  14.5 us (29%)
  waiting for transfers between devices  13.6 us (27%)
  other arithmetic  1.12 us (2%)
  local copies, waits for them, and re-layouts  0.98 us (2%)
  between operations  0.8 us (2%)
    ppermute x10, starting transfers between devices, swap(): lax.ppermute(block, axis, [(i, partner(i)) for i in range(lax.axis_size(a...  18.3 us
    ppermute x10, waiting for transfers between devices, swap(): lax.ppermute(block, axis, [(i, partner(i)) for i in range(lax.axis_size(a...  13.6 us
    pallas_call x1, Pallas kernels, remap(): pl.pallas_call(own_body, in_specs=[hbm, vmem], out_specs=vmem, out_shape=...  5.29 us
    pallas_call x1, Pallas kernels, remap(): pl.pallas_call(more_body, in_specs=[hbm, vmem], out_specs=[vmem, vmem], o...  2.88 us
    pallas_call x1, Pallas kernels, remap(): pl.pallas_call(prep_body, in_specs=[smem, smem] + [vmem] * 9 + [hbm, vmem...  2.62 us
    pallas_call x1, Pallas kernels, remap(): pl.pallas_call(load_body, in_specs=[hbm], out_specs=vmem, out_shape=block...  1.91 us
    pallas_call x1, Pallas kernels, remap(): pl.pallas_call(side_body, in_specs=[vmem, vmem], out_specs=vmem, out_shap...  1.78 us
    convert_element_type x1, other arithmetic, remap(): return (own + got_far.astype(F32) + got_near.astype(F32)).astype(BF16)  1 us
  transfers between devices with their start and end apart: 10, of which 5 were waited for; matrix products, arithmetic and copies ran while one was open for 0% of the time, Pallas kernels for 20%

profile of v3, /device:TPU:0, one launch (start us, length us, event | category | flops | bytes accessed | tf_op | source)
XLA Modules:
  0.0 49.4 jit_solution(16451876081234155424)
XLA Ops:
  0.0 0.9 %copy-done = bf16[16,32,256]{2,1,0:T(8,128)(2,1)S(1)} copy-done((bf16[16,32,256]{2,1,0:T(8,128)(2,1)S(1)}, bf16[16,32,256]{2,1,0:T(8,128)(2,1)}, u32[]{:S(2)}) %copy-start) | copy-done | bytes 262168
  1.0 0.1 edges.1
  1.0 0.1 collective-permute-start.1
  1.1 3.5 %collective-permute-start = (bf16[16,32,256]{2,1,0:T(8,128)(2,1)S(1)}, bf16[16,32,256]{2,1,0:T(8,128)(2,1)S(1)}, u32[]{:S(2)}, u32[]{:S(2)}) collective-permute-start(bf16[16,32,256]{2,1,0:T(8,128)(2,1)S(1)} %get-tuple-element.14.own), channel_id=1, source_target_pairs={{0,16},{8,24},{16,0},{24,8},{32,48},{40,56},{48,32},{56,40},{64,80... | collective-permute-start | bytes 786440 | tf_op jit(solution)/shard_map/ppermute | solution.py:17
  4.6 5.4 %collective-permute-start.2 = (bf16[16,256]{1,0:T(8,128)(2,1)S(1)}, bf16[16,256]{1,0:T(8,128)(2,1)S(1)}, u32[]{:S(2)}, u32[]{:S(2)}) collective-permute-start(bf16[16,256]{1,0:T(8,128)(2,1)S(1)} %get-tuple-element.15), channel_id=1, source_target_pairs={{0,7},{1,2},{2,1},{3,4},{4,3},{5,6},{6,5},{7,0},{8,15},{9,10},{10,... | collective-permute-start | bytes 24584 | tf_op jit(solution)/shard_map/ppermute | solution.py:17
  10.0 2.0 %collective-permute-done.2 = bf16[16,256]{1,0:T(8,128)(2,1)S(1)} collective-permute-done((bf16[16,256]{1,0:T(8,128)(2,1)S(1)}, bf16[16,256]{1,0:T(8,128)(2,1)S(1)}, u32[]{:S(2)}, u32[]{:S(2)}) %collective-permute-start.2) | collective-permute-done | bytes 8224 | tf_op jit(solution)/shard_map/ppermute | solution.py:17
  11.9 1.7 %collective-permute-done.3 = bf16[16,256]{1,0:T(8,128)(2,1)S(1)} collective-permute-done((bf16[16,256]{1,0:T(8,128)(2,1)S(1)}, bf16[16,256]{1,0:T(8,128)(2,1)S(1)}, u32[]{:S(2)}, u32[]{:S(2)}) %collective-permute-start.3) | collective-permute-done | bytes 8224 | tf_op jit(solution)/shard_map/ppermute | solution.py:17
  13.6 0.0 collective-permute-start.5
  13.6 3.4 %collective-permute-start.4 = (bf16[32,256]{1,0:T(8,128)(2,1)S(1)}, bf16[32,256]{1,0:T(8,128)(2,1)S(1)}, u32[]{:S(2)}, u32[]{:S(2)}) collective-permute-start(bf16[32,256]{1,0:T(8,128)(2,1)S(1)} %maximum_select_fusion.own_cols), channel_id=1, source_target_pairs={{0,16},{8,24},{16,0},{24,8},{32,48},{40,56},{48,32},{56,40},{64,80... | collective-permute-start | bytes 49160 | tf_op jit(solution)/shard_map/ppermute | solution.py:17
  17.0 0.1 select_dynamic-update-slice_fusion
  17.2 1.7 %collective-permute-done.4.near_cols = bf16[32,256]{1,0:T(8,128)(2,1)S(1)} collective-permute-done((bf16[32,256]{1,0:T(8,128)(2,1)S(1)}, bf16[32,256]{1,0:T(8,128)(2,1)S(1)}, u32[]{:S(2)}, u32[]{:S(2)}) %collective-permute-start.4) | collective-permute-done | bytes 16416 | tf_op jit(solution)/shard_map/ppermute | solution.py:17
  18.9 0.1 collective-permute-start.6
  19.0 1.9 %collective-permute-start.7 = (bf16[1,32,256]{2,1,0:T(8,128)(2,1)S(1)}, bf16[1,32,256]{2,1,0:T(8,128)(2,1)S(1)}, u32[]{:S(2)}, u32[]{:S(2)}) collective-permute-start(bf16[1,32,256]{2,1,0:T(8,128)(2,1)S(1)} %get-tuple-element.17), channel_id=1, source_target_pairs={{0,16},{8,32},{16,0},{24,48},{32,8},{40,64},{48,24},{56,80},{64,40... | collective-permute-start | bytes 49160 | tf_op jit(solution)/shard_map/ppermute | solution.py:17
  21.6 1.9 %load_far.1._ = bf16[1024,3072]{1,0:T(8,128)(2,1)S(1)} custom-call(bf16[3072,3072]{1,0:T(8,128)(2,1)} %bitcast.5), custom_call_target="tpu_custom_call" | custom-call | tf_op jit(solution)/shard_map/load_far/pallas_call | solution.py:192
  23.5 0.0 copy-start.1
  23.5 2.9 %load_more.1 = (bf16[1024,3072]{1,0:T(8,128)(2,1)S(1)}, bf16[1024,3072]{1,0:T(8,128)(2,1)S(1)}) custom-call(bf16[3072,3072]{1,0:T(8,128)(2,1)} %bitcast.6, bf16[1024,3072]{1,0:T(8,128)(2,1)S(1)} %load_far.1._), custom_call_target="tpu_custom_call", output_to_operand_aliasing={{0}: (1, {})} | custom-call | tf_op jit(solution)/shard_map/load_more/pallas_call | solution.py:201
  26.4 2.6 %prep.1 = (bf16[3072,256]{1,0:T(8,128)(2,1)S(1)}, bf16[1024,256]{1,0:T(8,128)(2,1)S(1)}, bf16[1024,3072]{1,0:T(8,128)(2,1)S(1)}) custom-call(s32[1,8]{1,0:T(1,128)S(1)} %copy-done.1, s32[1]{0:T(128)S(6)} %copy.13.counts, bf16[16,32,256]{2,1,0:T(8,128)(2,1)S(1)} %get-tuple-element.14.own, ...), custom_call_target="tpu_custom_call", output_to_operand_aliasing={{2}: (12, {})} | custom-call | tf_op jit(solution)/shard_map/prep/pallas_call | solution.py:230
  29.1 1.8 %side.1 = bf16[1024,256]{1,0:T(8,128)(2,1)S(1)} custom-call(bf16[1024,3072]{1,0:T(8,128)(2,1)S(1)} %get-tuple-element.22.w, bf16[3072,256]{1,0:T(8,128)(2,1)S(1)} %get-tuple-element.20.picked), custom_call_target="tpu_custom_call" | custom-call | tf_op jit(solution)/shard_map/side/pallas_call | solution.py:251
  30.9 0.1 collective-permute-start.9
  31.0 3.9 %collective-permute-start.8 = (bf16[1024,256]{1,0:T(8,128)(2,1)S(1)}, bf16[1024,256]{1,0:T(8,128)(2,1)S(1)}, u32[]{:S(2)}, u32[]{:S(2)}) collective-permute-start(bf16[1024,256]{1,0:T(8,128)(2,1)S(1)} %get-tuple-element.21), channel_id=1, source_target_pairs={{0,7},{1,2},{2,1},{3,4},{4,3},{5,6},{6,5},{7,0},{8,15},{9,10},{10,... | collective-permute-start | bytes 1572872 | tf_op jit(solution)/shard_map/ppermute | solution.py:17
  34.8 5.3 %own.1 = f32[1024,256]{1,0:T(8,128)S(1)} custom-call(bf16[3072,3072]{1,0:T(8,128)(2,1)} %bitcast.8, bf16[3072,256]{1,0:T(8,128)(2,1)S(1)} %get-tuple-element.20.picked), custom_call_target="tpu_custom_call" | custom-call | tf_op jit(solution)/shard_map/own/pallas_call | solution.py:260
  40.1 4.5 %collective-permute-done.9 = bf16[1024,256]{1,0:T(8,128)(2,1)S(1)} collective-permute-done((bf16[1024,256]{1,0:T(8,128)(2,1)S(1)}, bf16[1024,256]{1,0:T(8,128)(2,1)S(1)}, u32[]{:S(2)}, u32[]{:S(2)}) %collective-permute-start.9) | collective-permute-done | bytes 524320 | tf_op jit(solution)/shard_map/ppermute | solution.py:17
  44.7 3.7 %collective-permute-done.8 = bf16[1024,256]{1,0:T(8,128)(2,1)S(1)} collective-permute-done((bf16[1024,256]{1,0:T(8,128)(2,1)S(1)}, bf16[1024,256]{1,0:T(8,128)(2,1)S(1)}, u32[]{:S(2)}, u32[]{:S(2)}) %collective-permute-start.8) | collective-permute-done | bytes 524320 | tf_op jit(solution)/shard_map/ppermute | solution.py:17
  48.4 1.0 %add_convert_fusion = bf16[1024,256]{1,0:T(8,128)(2,1)} fusion(bf16[1024,256]{1,0:T(8,128)(2,1)S(1)} %collective-permute-done.9, f32[1024,256]{1,0:T(8,128)S(1)} %own.1, bf16[1024,256]{1,0:T(8,128)(2,1)S(1)} %collective-permute-done.8), kind=kLoop, calls=%fused_computation | loop fusion | flops 1310720 | bytes 2621440 | tf_op jit(solution)/shard_map/convert_element_type | solution.py:269
  (13 shorter events, 0.1 us)
Async XLA Ops:
  0.0 0.9 %copy-start = (bf16[16,32,256]{2,1,0:T(8,128)(2,1)S(1)}, bf16[16,32,256]{2,1,0:T(8,128)(2,1)}, u32[]{:S(2)}) copy-start(bf16[16,32,256]{2,1,0:T(8,128)(2,1)} %field.1) | copy-start | bytes 786436
  1.0 16.0 %collective-permute-start.1 = (bf16[16,32,256]{2,1,0:T(8,128)(2,1)S(1)}, bf16[16,32,256]{2,1,0:T(8,128)(2,1)S(1)}, u32[]{:S(2)}, u32[]{:S(2)}) collective-permute-start(bf16[16,32,256]{2,1,0:T(8,128)(2,1)S(1)} %get-tuple-element.14.own), channel_id=1, source_target_pairs={{0,8},{8,0},{16,32},{24,40},{32,16},{40,24},{48,64},{56,72},{64,48... | collective-permute-start | bytes 786440 | tf_op jit(solution)/shard_map/ppermute | solution.py:17
  1.1 15.9 %collective-permute-start = (bf16[16,32,256]{2,1,0:T(8,128)(2,1)S(1)}, bf16[16,32,256]{2,1,0:T(8,128)(2,1)S(1)}, u32[]{:S(2)}, u32[]{:S(2)}) collective-permute-start(bf16[16,32,256]{2,1,0:T(8,128)(2,1)S(1)} %get-tuple-element.14.own), channel_id=1, source_target_pairs={{0,16},{8,24},{16,0},{24,8},{32,48},{40,56},{48,32},{56,40},{64,80... | collective-permute-start | bytes 786440 | tf_op jit(solution)/shard_map/ppermute | solution.py:17
  4.6 7.4 %collective-permute-start.2 = (bf16[16,256]{1,0:T(8,128)(2,1)S(1)}, bf16[16,256]{1,0:T(8,128)(2,1)S(1)}, u32[]{:S(2)}, u32[]{:S(2)}) collective-permute-start(bf16[16,256]{1,0:T(8,128)(2,1)S(1)} %get-tuple-element.15), channel_id=1, source_target_pairs={{0,7},{1,2},{2,1},{3,4},{4,3},{5,6},{6,5},{7,0},{8,15},{9,10},{10,... | collective-permute-start | bytes 24584 | tf_op jit(solution)/shard_map/ppermute | solution.py:17
  10.0 3.7 %collective-permute-start.3 = (bf16[16,256]{1,0:T(8,128)(2,1)S(1)}, bf16[16,256]{1,0:T(8,128)(2,1)S(1)}, u32[]{:S(2)}, u32[]{:S(2)}) collective-permute-start(bf16[16,256]{1,0:T(8,128)(2,1)S(1)} %get-tuple-element.16), channel_id=1, source_target_pairs={{0,1},{1,0},{2,3},{3,2},{4,5},{5,4},{6,7},{7,6},{8,9},{9,8},{10,11... | collective-permute-start | bytes 24584 | tf_op jit(solution)/shard_map/ppermute | solution.py:17
  13.6 3.5 %collective-permute-start.5 = (bf16[32,256]{1,0:T(8,128)(2,1)S(1)}, bf16[32,256]{1,0:T(8,128)(2,1)S(1)}, u32[]{:S(2)}, u32[]{:S(2)}) collective-permute-start(bf16[32,256]{1,0:T(8,128)(2,1)S(1)} %maximum_select_fusion.own_cols), channel_id=1, source_target_pairs={{0,8},{8,0},{16,32},{24,40},{32,16},{40,24},{48,64},{56,72},{64,48... | collective-permute-start | bytes 49160 | tf_op jit(solution)/shard_map/ppermute | solution.py:17
  13.6 5.3 %collective-permute-start.4 = (bf16[32,256]{1,0:T(8,128)(2,1)S(1)}, bf16[32,256]{1,0:T(8,128)(2,1)S(1)}, u32[]{:S(2)}, u32[]{:S(2)}) collective-permute-start(bf16[32,256]{1,0:T(8,128)(2,1)S(1)} %maximum_select_fusion.own_cols), channel_id=1, source_target_pairs={{0,16},{8,24},{16,0},{24,8},{32,48},{40,56},{48,32},{56,40},{64,80... | collective-permute-start | bytes 49160 | tf_op jit(solution)/shard_map/ppermute | solution.py:17
  18.9 7.5 %collective-permute-start.6 = (bf16[35,32,256]{2,1,0:T(8,128)(2,1)S(1)}, bf16[35,32,256]{2,1,0:T(8,128)(2,1)S(1)}, u32[]{:S(2)}, u32[]{:S(2)}) collective-permute-start(bf16[35,32,256]{2,1,0:T(8,128)(2,1)S(1)} %fusion.2), channel_id=1, source_target_pairs={{0,8},{8,0},{16,24},{24,16},{32,40},{40,32},{48,56},{56,48},{64,72... | collective-permute-start | bytes 1720328 | tf_op jit(solution)/shard_map/ppermute | solution.py:17
  19.0 7.4 %collective-permute-start.7 = (bf16[1,32,256]{2,1,0:T(8,128)(2,1)S(1)}, bf16[1,32,256]{2,1,0:T(8,128)(2,1)S(1)}, u32[]{:S(2)}, u32[]{:S(2)}) collective-permute-start(bf16[1,32,256]{2,1,0:T(8,128)(2,1)S(1)} %get-tuple-element.17), channel_id=1, source_target_pairs={{0,16},{8,32},{16,0},{24,48},{32,8},{40,64},{48,24},{56,80},{64,40... | collective-permute-start | bytes 49160 | tf_op jit(solution)/shard_map/ppermute | solution.py:17
  23.5 2.9 %copy-start.1 = (s32[1,8]{1,0:T(1,128)S(1)}, s32[1,8]{1,0:T(1,128)}, u32[]{:S(2)}) copy-start(s32[1,8]{1,0:T(1,128)} %ids.1) | copy-start | bytes 100
  30.9 13.8 %collective-permute-start.9 = (bf16[1024,256]{1,0:T(8,128)(2,1)S(1)}, bf16[1024,256]{1,0:T(8,128)(2,1)S(1)}, u32[]{:S(2)}, u32[]{:S(2)}) collective-permute-start(bf16[1024,256]{1,0:T(8,128)(2,1)S(1)} %side.1), channel_id=1, source_target_pairs={{0,1},{1,0},{2,3},{3,2},{4,5},{5,4},{6,7},{7,6},{8,9},{9,8},{10,11... | collective-permute-start | bytes 1572872 | tf_op jit(solution)/shard_map/ppermute | solution.py:17
  31.0 17.4 %collective-permute-start.8 = (bf16[1024,256]{1,0:T(8,128)(2,1)S(1)}, bf16[1024,256]{1,0:T(8,128)(2,1)S(1)}, u32[]{:S(2)}, u32[]{:S(2)}) collective-permute-start(bf16[1024,256]{1,0:T(8,128)(2,1)S(1)} %get-tuple-element.21), channel_id=1, source_target_pairs={{0,7},{1,2},{2,1},{3,4},{4,3},{5,6},{6,5},{7,0},{8,15},{9,10},{10,... | collective-permute-start | bytes 1572872 | tf_op jit(solution)/shard_map/ppermute | solution.py:17

commit v4 on v3

--- a/solution.py
+++ b/solution.py
@@ -9,6 +9,8 @@
 SLOTS = 8
 REACH = 2
 CHUNKS = 4
+LEAD = 320
+EARLY = 384
 BF16 = jnp.bfloat16
 F32 = jnp.float32
 
@@ -46,18 +48,10 @@
     return w.at[pl.ds(top + first, count)]
 
 
-def load_body(w, far, sem):
-    half = far.shape[0] // 2
-    copy = pltpu.make_async_copy(rows_of(w, True, 0, half), far.at[pl.ds(0, half)], sem)
-    copy.start()
-    copy.wait()
-
-
-def more_body(w, _, far, near, sems):
-    half = far.shape[0] // 2
+def load_body(w, far, near, sems):
     copies = (
-        pltpu.make_async_copy(rows_of(w, True, half, half), far.at[pl.ds(half, half)], sems.at[0]),
-        pltpu.make_async_copy(rows_of(w, False, 0, half), near.at[pl.ds(0, half)], sems.at[1]),
+        pltpu.make_async_copy(rows_of(w, True, 0, far.shape[0]), far, sems.at[0]),
+        pltpu.make_async_copy(rows_of(w, False, 0, EARLY), near.at[pl.ds(0, EARLY)], sems.at[1]),
     )
     for copy in copies:
         copy.start()
@@ -65,9 +59,9 @@
         copy.wait()
 
 
-def prep_body(ids, counts, own, near, far, mate, beyond, own_cols, near_cols, far_cols, w, w_all, _, picked, out, w_near, rows, west, east, sem):
-    half = w_near.shape[0] // 2
-    coming = pltpu.make_async_copy(rows_of(w_all, False, half, half), w_near.at[pl.ds(half, half)], sem)
+def prep_body(ids, counts, own, near, far, hop, mate, beyond, own_cols, near_cols, far_cols, w, w_all, _, picked, out, w_near, rows, west, east, sem):
+    late = w_near.shape[0] - EARLY
+    coming = pltpu.make_async_copy(rows_of(w_all, False, EARLY, late), w_near.at[pl.ds(EARLY, late)], sem)
     coming.start()
     rows_per = own.shape[0]
     band = lax.axis_index("lat")
@@ -87,11 +81,11 @@
     place(REACH, own[...], own_cols[...].astype(F32))
     place(slot_of_near, near[...], near_cols[...].astype(F32))
     place(slot_of_far, far[...], far_cols[...].astype(F32))
-    place(slot_of_hop, mate[:rows_per], mate[2 * rows_per + 1].astype(F32))
-    place(slot_of_mate, mate[rows_per : 2 * rows_per], mate[2 * rows_per + 2].astype(F32))
+    place(slot_of_hop, hop[:rows_per], hop[rows_per + 1].astype(F32))
+    place(slot_of_mate, mate[...], hop[rows_per + 2].astype(F32))
     last = (2 * REACH + 1) * rows_per + 1
     rows[jnp.where(core == 0, 0, last)] = beyond[0]
-    rows[jnp.where(core == 0, last, 0)] = mate[2 * rows_per]
+    rows[jnp.where(core == 0, last, 0)] = hop[rows_per]
 
     @pl.when(band <= REACH)
     def _():
@@ -127,8 +121,10 @@
     coming.wait()
 
 
-def side_body(w, picked, out):
-    out[...] = jnp.dot(w[...], picked[...], preferred_element_type=F32).astype(BF16)
+def side_body(w, picked, out, *, first):
+    out[...] = jnp.dot(
+        w[first : first + out.shape[0]], picked[...], preferred_element_type=F32
+    ).astype(BF16)
 
 
 def own_body(w, picked, out, held, sems):
@@ -146,6 +142,18 @@
         copy.wait()
         here = slice(part * c, part * (c + 1))
         out[here] = jnp.dot(held[here], picked[...], preferred_element_type=F32)
+
+
+def join_body(own, far, near_a, near_b, out, ready, sems):
+    copies = []
+    for c, (first, near) in enumerate(((0, near_a), (LEAD, near_b))):
+        here = slice(first, first + near.shape[0])
+        ready[here] = (own[here] + far[here].astype(F32) + near[...].astype(F32)).astype(BF16)
+        span = pl.ds(first, near.shape[0])
+        copies.append(pltpu.make_async_copy(ready.at[span], out.at[span], sems.at[c]))
+        copies[-1].start()
+    for copy in copies:
+        copy.wait()
 
 
 def remap(field, weights, strip_ids, counts):
@@ -189,26 +197,17 @@
     width = w.shape[1]
 
     block = pltpu.VMEM((size, width), BF16)
-    w_far = pl.pallas_call(
+    w_far, w_near = pl.pallas_call(
         load_body,
         in_specs=[hbm],
-        out_specs=vmem,
-        out_shape=block,
-        scratch_shapes=[pltpu.SemaphoreType.DMA],
-        compiler_params=small,
-        name="load_far",
-    )(w)
-    w_far, w_near = pl.pallas_call(
-        more_body,
-        in_specs=[hbm, vmem],
         out_specs=[vmem, vmem],
         out_shape=[block, block],
         scratch_shapes=[pltpu.SemaphoreType.DMA((2,))],
-        input_output_aliases={1: 0},
         compiler_params=small,
-        name="load_more",
-    )(w, held(w_far))
-
+        name="load",
+    )(w)
+
+    mate = swap(tile, "lat", lambda i: i ^ 1)
     pick_near = core == odd
     other_rows = jnp.where(
         core == 0,
@@ -218,19 +217,18 @@
     message = jnp.concatenate(
         [
             jnp.where(pick_near, near, far),
-            tile,
             other_rows,
             jnp.where(pick_near, near_cols, far_cols)[None],
             cols[None],
         ]
     )
-    mate = swap(message, "lat", lambda i: i ^ 1)
+    hop = swap(message, "lat", lambda i: i ^ 1)
 
     halo = (2 * REACH + 1) * rows_per
     picked, to_far, w_near = pl.pallas_call(
         prep_body,
-        in_specs=[smem, smem] + [vmem] * 9 + [hbm, vmem],
-        input_output_aliases={12: 2},
+        in_specs=[smem, smem] + [vmem] * 10 + [hbm, vmem],
+        input_output_aliases={13: 2},
         out_specs=[vmem] * 3,
         out_shape=[
             pltpu.VMEM((width, chan), BF16),
@@ -245,18 +243,23 @@
         ],
         compiler_params=pltpu.CompilerParams(vmem_limit_bytes=16 << 20),
         name="prep",
-    )(strip_ids, counts, held(tile), near, far, mate, beyond, cols, near_cols, far_cols, held(w_far), w, held(w_near))
+    )(strip_ids, counts, held(tile), near, far, hop, mate, beyond, cols, near_cols, far_cols, held(w_far), w, held(w_near))
     picked = held(picked)
     got_far = swap(to_far, "lon", far_lon)
-    to_near = pl.pallas_call(
-        side_body,
-        in_specs=[vmem, vmem],
-        out_specs=vmem,
-        out_shape=pltpu.VMEM((size, chan), BF16),
-        compiler_params=pltpu.CompilerParams(vmem_limit_bytes=16 << 20),
-        name="side",
-    )(held(w_near), picked)
-    got_near = swap(to_near, "lon", near_lon)
+    w_near = held(w_near)
+
+    def side(first, count):
+        return pl.pallas_call(
+            lambda *refs: side_body(*refs, first=first),
+            in_specs=[vmem, vmem],
+            out_specs=vmem,
+            out_shape=pltpu.VMEM((count, chan), BF16),
+            compiler_params=pltpu.CompilerParams(vmem_limit_bytes=16 << 20),
+        )(w_near, picked)
+
+    got_near = [
+        swap(side(0, LEAD), "lon", near_lon), swap(side(LEAD, size - LEAD), "lon", near_lon)
+    ]
     own = pl.pallas_call(
         own_body,
         in_specs=[hbm, vmem],
@@ -266,7 +269,15 @@
         compiler_params=pltpu.CompilerParams(vmem_limit_bytes=16 << 20),
         name="own",
     )(w, picked)
-    return (own + got_far.astype(F32) + got_near.astype(F32)).astype(BF16)
+    return pl.pallas_call(
+        join_body,
+        in_specs=[vmem] * 4,
+        out_specs=hbm,
+        out_shape=jax.ShapeDtypeStruct((size, chan), BF16),
+        scratch_shapes=[pltpu.VMEM((size, chan), BF16), pltpu.SemaphoreType.DMA((2,))],
+        compiler_params=pltpu.CompilerParams(vmem_limit_bytes=4 << 20),
+        name="join",
+    )(held(own), got_far, *got_near)
 
 
 def solution(mesh):

time: 49.5 us -> 50.2 us (1.014)
  the two profiles are of different devices: /device:TPU:0 before, /device:TPU:1 now
where the time goes in v4:
time: 50.2 us; the launch traced here: 50 us
  starting transfers between devices  18.3 us (36%)
  waiting for transfers between devices  15.4 us (31%)
  Pallas kernels  14.5 us (29%)
  local copies, waits for them, and re-layouts  0.96 us (2%)
  between operations  0.78 us (2%)
    ppermute x12, starting transfers between devices, swap(): lax.ppermute(block, axis, [(i, partner(i)) for i in range(lax.axis_size(a...  18.3 us
    ppermute x12, waiting for transfers between devices, swap(): lax.ppermute(block, axis, [(i, partner(i)) for i in range(lax.axis_size(a...  15.4 us
    pallas_call x1, Pallas kernels, remap(): pl.pallas_call(own_body, in_specs=[hbm, vmem], out_specs=vmem, out_shape=...  5.29 us
    pallas_call x1, Pallas kernels, remap(): pl.pallas_call(load_body, in_specs=[hbm], out_specs=[vmem, vmem], out_sha...  3.52 us
    pallas_call x1, Pallas kernels, remap(): pl.pallas_call(prep_body, in_specs=[smem, smem] + [vmem] * 10 + [hbm, vme...  2.72 us
    pallas_call x2, Pallas kernels, side(): pl.pallas_call(lambda *refs: side_body(*refs, first=first), in_specs=[vme...  1.95 us
  transfers between devices with their start and end apart: 12, of which 3 were waited for; matrix products, arithmetic and copies ran while one was open for 0% of the time, Pallas kernels for 22%

profile of v4, /device:TPU:1, one launch (start us, length us, event | category | flops | bytes accessed | tf_op | source)
XLA Modules:
  0.0 50.0 jit_solution(1497748786849254958)
XLA Ops:
  0.0 0.9 %copy-done = bf16[16,32,256]{2,1,0:T(8,128)(2,1)S(1)} copy-done((bf16[16,32,256]{2,1,0:T(8,128)(2,1)S(1)}, bf16[16,32,256]{2,1,0:T(8,128)(2,1)}, u32[]{:S(2)}) %copy-start) | copy-done | bytes 262168
  1.0 0.1 edges.1
  1.0 6.0 %collective-permute-start.2 = (bf16[16,256]{1,0:T(8,128)(2,1)S(1)}, bf16[16,256]{1,0:T(8,128)(2,1)S(1)}, u32[]{:S(2)}, u32[]{:S(2)}) collective-permute-start(bf16[16,256]{1,0:T(8,128)(2,1)S(1)} %get-tuple-element.15), channel_id=1, source_target_pairs={{0,7},{1,2},{2,1},{3,4},{4,3},{5,6},{6,5},{7,0},{8,15},{9,10},{10,... | collective-permute-start | bytes 24584 | tf_op jit(solution)/shard_map/ppermute | solution.py:19
  7.0 1.0 %collective-permute-start.1 = (bf16[16,32,256]{2,1,0:T(8,128)(2,1)S(1)}, bf16[16,32,256]{2,1,0:T(8,128)(2,1)S(1)}, u32[]{:S(2)}, u32[]{:S(2)}) collective-permute-start(bf16[16,32,256]{2,1,0:T(8,128)(2,1)S(1)} %get-tuple-element.14.own), channel_id=1, source_target_pairs={{0,8},{8,0},{16,32},{24,40},{32,16},{40,24},{48,64},{56,72},{64,48... | collective-permute-start | bytes 786440 | tf_op jit(solution)/shard_map/ppermute | solution.py:19
  8.0 1.9 %collective-permute-start = (bf16[16,32,256]{2,1,0:T(8,128)(2,1)S(1)}, bf16[16,32,256]{2,1,0:T(8,128)(2,1)S(1)}, u32[]{:S(2)}, u32[]{:S(2)}) collective-permute-start(bf16[16,32,256]{2,1,0:T(8,128)(2,1)S(1)} %get-tuple-element.14.own), channel_id=1, source_target_pairs={{0,16},{8,24},{16,0},{24,8},{32,48},{40,56},{48,32},{56,40},{64,80... | collective-permute-start | bytes 786440 | tf_op jit(solution)/shard_map/ppermute | solution.py:19
  9.9 1.8 %collective-permute-start.5 = (bf16[32,256]{1,0:T(8,128)(2,1)S(1)}, bf16[32,256]{1,0:T(8,128)(2,1)S(1)}, u32[]{:S(2)}, u32[]{:S(2)}) collective-permute-start(bf16[32,256]{1,0:T(8,128)(2,1)S(1)} %maximum_select_fusion.own_cols), channel_id=1, source_target_pairs={{0,8},{8,0},{16,32},{24,40},{32,16},{40,24},{48,64},{56,72},{64,48... | collective-permute-start | bytes 49160 | tf_op jit(solution)/shard_map/ppermute | solution.py:19
  11.6 1.1 %collective-permute-start.4 = (bf16[32,256]{1,0:T(8,128)(2,1)S(1)}, bf16[32,256]{1,0:T(8,128)(2,1)S(1)}, u32[]{:S(2)}, u32[]{:S(2)}) collective-permute-start(bf16[32,256]{1,0:T(8,128)(2,1)S(1)} %maximum_select_fusion.own_cols), channel_id=1, source_target_pairs={{0,16},{8,24},{16,0},{24,8},{32,48},{40,56},{48,32},{56,40},{64,80... | collective-permute-start | bytes 49160 | tf_op jit(solution)/shard_map/ppermute | solution.py:19
  12.8 8.8 %collective-permute-done.4.near_cols = bf16[32,256]{1,0:T(8,128)(2,1)S(1)} collective-permute-done((bf16[32,256]{1,0:T(8,128)(2,1)S(1)}, bf16[32,256]{1,0:T(8,128)(2,1)S(1)}, u32[]{:S(2)}, u32[]{:S(2)}) %collective-permute-start.4) | collective-permute-done | bytes 16416 | tf_op jit(solution)/shard_map/ppermute | solution.py:19
  21.7 0.1 pad_maximum_fusion
  21.7 1.9 %collective-permute-start.6 = (bf16[19,32,256]{2,1,0:T(8,128)(2,1)S(1)}, bf16[19,32,256]{2,1,0:T(8,128)(2,1)S(1)}, u32[]{:S(2)}, u32[]{:S(2)}) collective-permute-start(bf16[19,32,256]{2,1,0:T(8,128)(2,1)S(1)} %pad_maximum_fusion), channel_id=1, source_target_pairs={{0,8},{8,0},{16,24},{24,16},{32,40},{40,32},{48,56},{56,48},{64,72... | collective-permute-start | bytes 933896 | tf_op jit(solution)/shard_map/ppermute | solution.py:19
  23.6 0.1 collective-permute-start.7
  23.7 1.9 %collective-permute-start.8 = (bf16[1,32,256]{2,1,0:T(8,128)(2,1)S(1)}, bf16[1,32,256]{2,1,0:T(8,128)(2,1)S(1)}, u32[]{:S(2)}, u32[]{:S(2)}) collective-permute-start(bf16[1,32,256]{2,1,0:T(8,128)(2,1)S(1)} %get-tuple-element.17), channel_id=1, source_target_pairs={{0,16},{8,32},{16,0},{24,48},{32,8},{40,64},{48,24},{56,80},{64,40... | collective-permute-start | bytes 49160 | tf_op jit(solution)/shard_map/ppermute | solution.py:19
  26.3 0.0 copy-start.1
  26.3 3.5 %load.1 = (bf16[1024,3072]{1,0:T(8,128)(2,1)S(1)}, bf16[1024,3072]{1,0:T(8,128)(2,1)S(1)}) custom-call(bf16[3072,3072]{1,0:T(8,128)(2,1)} %bitcast.5), custom_call_target="tpu_custom_call" | custom-call | tf_op jit(solution)/shard_map/load/pallas_call | solution.py:200
  29.9 2.7 %prep.1 = (bf16[3072,256]{1,0:T(8,128)(2,1)S(1)}, bf16[1024,256]{1,0:T(8,128)(2,1)S(1)}, bf16[1024,3072]{1,0:T(8,128)(2,1)S(1)}) custom-call(s32[1,8]{1,0:T(1,128)S(1)} %copy-done.1, s32[1]{0:T(128)S(6)} %copy.7.counts, bf16[16,32,256]{2,1,0:T(8,128)(2,1)S(1)} %get-tuple-element.14.own, ...), custom_call_target="tpu_custom_call", output_to_operand_aliasing={{2}: (13, {})} | custom-call | tf_op jit(solution)/shard_map/prep/pallas_call | solution.py:228
  32.6 1.1 %collective-permute-start.9 = (bf16[1024,256]{1,0:T(8,128)(2,1)S(1)}, bf16[1024,256]{1,0:T(8,128)(2,1)S(1)}, u32[]{:S(2)}, u32[]{:S(2)}) collective-permute-start(bf16[1024,256]{1,0:T(8,128)(2,1)S(1)} %get-tuple-element.21), channel_id=1, source_target_pairs={{0,7},{1,2},{2,1},{3,4},{4,3},{5,6},{6,5},{7,0},{8,15},{9,10},{10,... | collective-permute-start | bytes 1572872 | tf_op jit(solution)/shard_map/ppermute | solution.py:19
  33.7 1.3 %shard_map.47 = bf16[704,256]{1,0:T(8,128)(2,1)S(1)} custom-call(bf16[1024,3072]{1,0:T(8,128)(2,1)S(1)} %get-tuple-element.22.refs_0_, bf16[3072,256]{1,0:T(8,128)(2,1)S(1)} %get-tuple-element.20.picked.refs_1_), custom_call_target="tpu_custom_call" | custom-call | tf_op jit(solution)/shard_map/pallas_call | solution.py:252
  35.0 0.6 %collective-permute-start.11 = (bf16[704,256]{1,0:T(8,128)(2,1)S(1)}, bf16[704,256]{1,0:T(8,128)(2,1)S(1)}, u32[]{:S(2)}, u32[]{:S(2)}) collective-permute-start(bf16[704,256]{1,0:T(8,128)(2,1)S(1)} %shard_map.47), channel_id=1, source_target_pairs={{0,1},{1,0},{2,3},{3,2},{4,5},{5,4},{6,7},{7,6},{8,9},{9,8},{10,11... | collective-permute-start | bytes 1081352 | tf_op jit(solution)/shard_map/ppermute | solution.py:19
  35.5 0.7 %shard_map.46 = bf16[320,256]{1,0:T(8,128)(2,1)S(1)} custom-call(bf16[1024,3072]{1,0:T(8,128)(2,1)S(1)} %get-tuple-element.22.refs_0_, bf16[3072,256]{1,0:T(8,128)(2,1)S(1)} %get-tuple-element.20.picked.refs_1_), custom_call_target="tpu_custom_call" | custom-call | tf_op jit(solution)/shard_map/pallas_call | solution.py:252
  36.2 1.0 %collective-permute-start.10 = (bf16[320,256]{1,0:T(8,128)(2,1)S(1)}, bf16[320,256]{1,0:T(8,128)(2,1)S(1)}, u32[]{:S(2)}, u32[]{:S(2)}) collective-permute-start(bf16[320,256]{1,0:T(8,128)(2,1)S(1)} %shard_map.46), channel_id=1, source_target_pairs={{0,1},{1,0},{2,3},{3,2},{4,5},{5,4},{6,7},{7,6},{8,9},{9,8},{10,11... | collective-permute-start | bytes 491528 | tf_op jit(solution)/shard_map/ppermute | solution.py:19
  37.3 5.3 %own.1 = f32[1024,256]{1,0:T(8,128)S(1)} custom-call(bf16[3072,3072]{1,0:T(8,128)(2,1)} %bitcast.7, bf16[3072,256]{1,0:T(8,128)(2,1)S(1)} %get-tuple-element.20.picked.refs_1_), custom_call_target="tpu_custom_call" | custom-call | tf_op jit(solution)/shard_map/own/pallas_call | solution.py:263
  42.6 6.3 %collective-permute-done.10.near_a = bf16[320,256]{1,0:T(8,128)(2,1)S(1)} collective-permute-done((bf16[320,256]{1,0:T(8,128)(2,1)S(1)}, bf16[320,256]{1,0:T(8,128)(2,1)S(1)}, u32[]{:S(2)}, u32[]{:S(2)}) %collective-permute-start.10) | collective-permute-done | bytes 163872 | tf_op jit(solution)/shard_map/ppermute | solution.py:19
  48.9 0.2 collective-permute-done.9.far
  49.1 0.9 %join.1 = bf16[1024,256]{1,0:T(8,128)(2,1)} custom-call(f32[1024,256]{1,0:T(8,128)S(1)} %own.1, bf16[1024,256]{1,0:T(8,128)(2,1)S(1)} %collective-permute-done.9.far, bf16[320,256]{1,0:T(8,128)(2,1)S(1)} %collective-permute-done.10.near_a, bf16[704,256]{1,0:T(8,128)(2,1)S(1)} %collective-permute-done.11.near_b), custom_call_target="tpu_custom_call" | custom-call | tf_op jit(solution)/shard_map/join/pallas_call | solution.py:272
  (17 shorter events, 0.1 us)
Async XLA Ops:
  0.0 0.9 %copy-start = (bf16[16,32,256]{2,1,0:T(8,128)(2,1)S(1)}, bf16[16,32,256]{2,1,0:T(8,128)(2,1)}, u32[]{:S(2)}) copy-start(bf16[16,32,256]{2,1,0:T(8,128)(2,1)} %field.1) | copy-start | bytes 786436
  1.0 8.8 %collective-permute-start.2 = (bf16[16,256]{1,0:T(8,128)(2,1)S(1)}, bf16[16,256]{1,0:T(8,128)(2,1)S(1)}, u32[]{:S(2)}, u32[]{:S(2)}) collective-permute-start(bf16[16,256]{1,0:T(8,128)(2,1)S(1)} %get-tuple-element.15), channel_id=1, source_target_pairs={{0,7},{1,2},{2,1},{3,4},{4,3},{5,6},{6,5},{7,0},{8,15},{9,10},{10,... | collective-permute-start | bytes 24584 | tf_op jit(solution)/shard_map/ppermute | solution.py:19
  7.0 2.8 %collective-permute-start.3 = (bf16[16,256]{1,0:T(8,128)(2,1)S(1)}, bf16[16,256]{1,0:T(8,128)(2,1)S(1)}, u32[]{:S(2)}, u32[]{:S(2)}) collective-permute-start(bf16[16,256]{1,0:T(8,128)(2,1)S(1)} %get-tuple-element.16), channel_id=1, source_target_pairs={{0,1},{1,0},{2,3},{3,2},{4,5},{5,4},{6,7},{7,6},{8,9},{9,8},{10,11... | collective-permute-start | bytes 24584 | tf_op jit(solution)/shard_map/ppermute | solution.py:19
  7.0 14.6 %collective-permute-start.1 = (bf16[16,32,256]{2,1,0:T(8,128)(2,1)S(1)}, bf16[16,32,256]{2,1,0:T(8,128)(2,1)S(1)}, u32[]{:S(2)}, u32[]{:S(2)}) collective-permute-start(bf16[16,32,256]{2,1,0:T(8,128)(2,1)S(1)} %get-tuple-element.14.own), channel_id=1, source_target_pairs={{0,8},{8,0},{16,32},{24,40},{32,16},{40,24},{48,64},{56,72},{64,48... | collective-permute-start | bytes 786440 | tf_op jit(solution)/shard_map/ppermute | solution.py:19
  8.0 13.6 %collective-permute-start = (bf16[16,32,256]{2,1,0:T(8,128)(2,1)S(1)}, bf16[16,32,256]{2,1,0:T(8,128)(2,1)S(1)}, u32[]{:S(2)}, u32[]{:S(2)}) collective-permute-start(bf16[16,32,256]{2,1,0:T(8,128)(2,1)S(1)} %get-tuple-element.14.own), channel_id=1, source_target_pairs={{0,16},{8,24},{16,0},{24,8},{32,48},{40,56},{48,32},{56,40},{64,80... | collective-permute-start | bytes 786440 | tf_op jit(solution)/shard_map/ppermute | solution.py:19
  9.9 2.9 %collective-permute-start.5 = (bf16[32,256]{1,0:T(8,128)(2,1)S(1)}, bf16[32,256]{1,0:T(8,128)(2,1)S(1)}, u32[]{:S(2)}, u32[]{:S(2)}) collective-permute-start(bf16[32,256]{1,0:T(8,128)(2,1)S(1)} %maximum_select_fusion.own_cols), channel_id=1, source_target_pairs={{0,8},{8,0},{16,32},{24,40},{32,16},{40,24},{48,64},{56,72},{64,48... | collective-permute-start | bytes 49160 | tf_op jit(solution)/shard_map/ppermute | solution.py:19
  11.6 10.0 %collective-permute-start.4 = (bf16[32,256]{1,0:T(8,128)(2,1)S(1)}, bf16[32,256]{1,0:T(8,128)(2,1)S(1)}, u32[]{:S(2)}, u32[]{:S(2)}) collective-permute-start(bf16[32,256]{1,0:T(8,128)(2,1)S(1)} %maximum_select_fusion.own_cols), channel_id=1, source_target_pairs={{0,16},{8,24},{16,0},{24,8},{32,48},{40,56},{48,32},{56,40},{64,80... | collective-permute-start | bytes 49160 | tf_op jit(solution)/shard_map/ppermute | solution.py:19
  21.7 8.1 %collective-permute-start.6 = (bf16[19,32,256]{2,1,0:T(8,128)(2,1)S(1)}, bf16[19,32,256]{2,1,0:T(8,128)(2,1)S(1)}, u32[]{:S(2)}, u32[]{:S(2)}) collective-permute-start(bf16[19,32,256]{2,1,0:T(8,128)(2,1)S(1)} %pad_maximum_fusion), channel_id=1, source_target_pairs={{0,8},{8,0},{16,24},{24,16},{32,40},{40,32},{48,56},{56,48},{64,72... | collective-permute-start | bytes 933896 | tf_op jit(solution)/shard_map/ppermute | solution.py:19
  23.6 6.2 %collective-permute-start.7 = (bf16[16,32,256]{2,1,0:T(8,128)(2,1)S(1)}, bf16[16,32,256]{2,1,0:T(8,128)(2,1)S(1)}, u32[]{:S(2)}, u32[]{:S(2)}) collective-permute-start(bf16[16,32,256]{2,1,0:T(8,128)(2,1)S(1)} %get-tuple-element.14.own), channel_id=1, source_target_pairs={{0,8},{8,0},{16,24},{24,16},{32,40},{40,32},{48,56},{56,48},{64,72... | collective-permute-start | bytes 786440 | tf_op jit(solution)/shard_map/ppermute | solution.py:19
  23.7 6.1 %collective-permute-start.8 = (bf16[1,32,256]{2,1,0:T(8,128)(2,1)S(1)}, bf16[1,32,256]{2,1,0:T(8,128)(2,1)S(1)}, u32[]{:S(2)}, u32[]{:S(2)}) collective-permute-start(bf16[1,32,256]{2,1,0:T(8,128)(2,1)S(1)} %get-tuple-element.17), channel_id=1, source_target_pairs={{0,16},{8,32},{16,0},{24,48},{32,8},{40,64},{48,24},{56,80},{64,40... | collective-permute-start | bytes 49160 | tf_op jit(solution)/shard_map/ppermute | solution.py:19
  26.3 3.6 %copy-start.1 = (s32[1,8]{1,0:T(1,128)S(1)}, s32[1,8]{1,0:T(1,128)}, u32[]{:S(2)}) copy-start(s32[1,8]{1,0:T(1,128)} %ids.1) | copy-start | bytes 100
  32.6 16.5 %collective-permute-start.9 = (bf16[1024,256]{1,0:T(8,128)(2,1)S(1)}, bf16[1024,256]{1,0:T(8,128)(2,1)S(1)}, u32[]{:S(2)}, u32[]{:S(2)}) collective-permute-start(bf16[1024,256]{1,0:T(8,128)(2,1)S(1)} %get-tuple-element.21), channel_id=1, source_target_pairs={{0,7},{1,2},{2,1},{3,4},{4,3},{5,6},{6,5},{7,0},{8,15},{9,10},{10,... | collective-permute-start | bytes 1572872 | tf_op jit(solution)/shard_map/ppermute | solution.py:19
  35.0 13.9 %collective-permute-start.11 = (bf16[704,256]{1,0:T(8,128)(2,1)S(1)}, bf16[704,256]{1,0:T(8,128)(2,1)S(1)}, u32[]{:S(2)}, u32[]{:S(2)}) collective-permute-start(bf16[704,256]{1,0:T(8,128)(2,1)S(1)} %shard_map.47), channel_id=1, source_target_pairs={{0,1},{1,0},{2,3},{3,2},{4,5},{5,4},{6,7},{7,6},{8,9},{9,8},{10,11... | collective-permute-start | bytes 1081352 | tf_op jit(solution)/shard_map/ppermute | solution.py:19
  36.2 12.7 %collective-permute-start.10 = (bf16[320,256]{1,0:T(8,128)(2,1)S(1)}, bf16[320,256]{1,0:T(8,128)(2,1)S(1)}, u32[]{:S(2)}, u32[]{:S(2)}) collective-permute-start(bf16[320,256]{1,0:T(8,128)(2,1)S(1)} %shard_map.46), channel_id=1, source_target_pairs={{0,1},{1,0},{2,3},{3,2},{4,5},{5,4},{6,7},{7,6},{8,9},{9,8},{10,11... | collective-permute-start | bytes 491528 | tf_op jit(solution)/shard_map/ppermute | solution.py:19
